TPU v7x, 32 devices: a whole 2x2x4 slice. The times are simulated.
32 devices in a mesh: dp: 16 (over z, x, core), mp: 2 (over y).
Axes of the slice: x: 2, y: 2, z: 4, core: 2. Of those that a mesh axis runs over, the one named last changes fastest.
Arguments:
- tokens: bfloat16 [8192, 8192], P('dp'), may hold values from -6 to 6
- queries: bfloat16 [8192, 64, 128], P('dp', 'mp'), may hold values from -68 to 68
- out_grad: bfloat16 [8192, 64, 128], P('dp', 'mp'), may hold values from -6 to 6
- segment_ids: int32 [16, 512], P('dp'), may hold values from 0 to 3, never falling along the last dimension, each value on 1 to 256 neighbouring positions
- weight_slots: bfloat16 [16384, 8, 2, 128], P('dp', 'mp'), may hold values from -0.0625 to 0.0625
- old_place: int32 [64], replicated, may hold values from 0 to 127, as said below
- new_place: int32 [64], replicated, may hold values from 0 to 127, as said below
Outputs:
- input_grad: bfloat16 [8192, 8192], P('dp', 'mp')
- query_grad: bfloat16 [8192, 64, 128], P('dp', 'mp')
- weight_grad: float32 [16384, 8, 2, 128], P('dp', 'mp')
Inputs may be any that keep to these rules, and one draw needn't show every extreme that they name: `old_place`: entries are distinct slot numbers; slot s lies on index s // 8 of dp; some index of dp holds 8 blocks. `new_place`: entries are distinct slot numbers; slot s lies on index s // 8 of dp; some index of dp receives 8 blocks.
All inputs are finite; a program needn't handle non-finite values.
Results may differ from a plain program's by a relative error of at most 0.018.
Values may be sent and summed in bfloat16 or wider, within the bound.
A program may use at most 192 MiB of HBM per device.

v0:
```python
import functools

import jax
import jax.numpy as jnp
from jax import lax
from jax.experimental import pallas as pl
from jax.experimental.pallas import tpu as pltpu
from jax.sharding import PartitionSpec as P

BR = 128
LOG2E = 1.4426950408889634
VMEM_LIMIT = 60 * 1024 * 1024


def params():
    return pltpu.CompilerParams(
        dimension_semantics=("arbitrary",), vmem_limit_bytes=VMEM_LIMIT
    )


def group_of(count):
    for size in (8, 4, 2):
        if count % size == 0:
            return size
    return 1


def block_specs(group, width):
    return [
        pl.BlockSpec((BR, width), functools.partial(lambda r, i, p: (p[i * group + r], 0), r))
        for r in range(group)
    ]


def project_kernel(group, head_size, place, tok_ref, cos_ref, sin_ref, *refs):
    blocks, out_ref, total = refs[:group], refs[group], refs[group + 1]
    step = pl.program_id(0)

    @pl.when(step == 0)
    def _():
        total[...] = jnp.zeros_like(total)

    w = jnp.concatenate([b[...] for b in blocks], axis=0)
    total[...] += jnp.dot(tok_ref[...], w, preferred_element_type=jnp.float32)

    @pl.when(step == pl.num_programs(0) - 1)
    def _():
        pair = 2 * head_size
        for h in range(total.shape[1] // pair):
            key = total[:, h * pair : h * pair + head_size]
            rot = key * cos_ref[...] + pltpu.roll(key, head_size // 2, 1) * sin_ref[...]
            out_ref[:, h * pair : h * pair + head_size] = rot.astype(jnp.bfloat16)
            value = total[:, h * pair + head_size : (h + 1) * pair]
            out_ref[:, h * pair + head_size : (h + 1) * pair] = value.astype(jnp.bfloat16)


def project(tokens, gathered, place, cos_tab, sin_tab, head_size):
    tok_count = tokens.shape[0]
    width = gathered.shape[1]
    count = place.shape[0]
    group = group_of(count)
    table = pl.BlockSpec((tok_count, head_size), lambda i, p: (0, 0))
    return pl.pallas_call(
        functools.partial(project_kernel, group, head_size),
        out_shape=jax.ShapeDtypeStruct((tok_count, width), jnp.bfloat16),
        grid_spec=pltpu.PrefetchScalarGridSpec(
            num_scalar_prefetch=1,
            grid=(count // group,),
            in_specs=[pl.BlockSpec((tok_count, group * BR), lambda i, p: (0, i)), table, table]
            + block_specs(group, width),
            out_specs=pl.BlockSpec((tok_count, width), lambda i, p: (0, 0)),
            scratch_shapes=[pltpu.VMEM((tok_count, width), jnp.float32)],
        ),
        compiler_params=params(),
        cost_estimate=pl.CostEstimate(
            flops=2 * tok_count * count * BR * width,
            bytes_accessed=2 * (tok_count * count * BR + count * BR * width + tok_count * width),
            transcendentals=0,
        ),
        name="project",
    )(place, tokens, cos_tab, sin_tab, *([gathered] * group))


def attend_kernel(
    per_head, tile, q_ref, og_ref, kv_ref, col_ref, row_ref, cos_ref, sin_ref,
    dq_ref, pair_ref, bias, key_t, rot_acc, val_acc,
):
    tok_count, pair = kv_ref.shape
    hd = pair // 2
    inv_root = 1.0 / (hd ** 0.5)

    @pl.when(pl.program_id(0) == 0)
    def _():
        kpos = lax.broadcasted_iota(jnp.int32, bias.shape, 0)
        qpos = lax.broadcasted_iota(jnp.int32, bias.shape, 1)
        allowed = (kpos <= qpos) & (col_ref[...] == row_ref[...])
        bias[...] = jnp.where(allowed, 0.0, -1e30).astype(jnp.float32)

    key_t[...] = kv_ref[:, :hd].astype(jnp.float32).T.astype(jnp.bfloat16)
    rot_acc[...] = jnp.zeros_like(rot_acc)
    val_acc[...] = jnp.zeros_like(val_acc)

    def head(j, carry):
        lanes = pl.ds(pl.multiple_of(j * hd, hd), hd)
        for t in range(tok_count // tile):
            rows = slice(t * tile, (t + 1) * tile)
            reach = (t + 1) * tile
            q = q_ref[rows, lanes]
            og = og_ref[rows, lanes]
            nt = (((1,), (1,)), ((), ()))
            s = lax.dot_general(kv_ref[:reach, :hd], q, nt, preferred_element_type=jnp.float32)
            s = s * (inv_root * LOG2E) + bias[:reach, rows]
            e = jnp.exp2(s - jnp.max(s, axis=0, keepdims=True))
            p = e * (1.0 / jnp.sum(e, axis=0, keepdims=True))
            pb = p.astype(jnp.bfloat16)
            dp = lax.dot_general(kv_ref[:reach, hd:], og, nt, preferred_element_type=jnp.float32)
            dot = jnp.sum(pb.astype(jnp.float32) * dp, axis=0, keepdims=True)
            ds = (p * (dp - dot)).astype(jnp.bfloat16)
            val_acc[:reach, :] += jnp.dot(pb, og, preferred_element_type=jnp.float32)
            rot_acc[:reach, :] += jnp.dot(ds, q, preferred_element_type=jnp.float32)
            dq = jnp.dot(key_t[:, :reach], ds, preferred_element_type=jnp.float32)
            dq_ref[rows, lanes] = (dq * inv_root).T.astype(jnp.bfloat16)
        return carry

    lax.fori_loop(0, per_head, head, 0, unroll=2)
    g = rot_acc[...] * inv_root
    back = g * cos_ref[...] - pltpu.roll(g, hd // 2, 1) * sin_ref[...]
    pair_ref[:, :hd] = back.astype(jnp.bfloat16)
    pair_ref[:, hd:] = val_acc[...].astype(jnp.bfloat16)


def attend(queries, out_grad, pairs, seg_row, cos_tab, sin_tab, head_count, head_size):
    tok_count, q_width = queries.shape
    per_head = q_width // head_count // head_size
    tile = tok_count // 2 if tok_count % 512 == 0 else tok_count
    slab = pl.BlockSpec((tok_count, per_head * head_size), lambda h: (0, h))
    both = pl.BlockSpec((tok_count, 2 * head_size), lambda h: (0, h))
    table = pl.BlockSpec((tok_count, head_size), lambda h: (0, 0))
    col = pl.BlockSpec((tok_count, 1), lambda h: (0, 0))
    row = pl.BlockSpec((1, tok_count), lambda h: (0, 0))
    return pl.pallas_call(
        functools.partial(attend_kernel, per_head, tile),
        out_shape=(
            jax.ShapeDtypeStruct(queries.shape, jnp.bfloat16),
            jax.ShapeDtypeStruct(pairs.shape, jnp.bfloat16),
        ),
        grid=(head_count,),
        in_specs=[slab, slab, both, col, row, table, table],
        out_specs=(slab, both),
        scratch_shapes=[
            pltpu.VMEM((tok_count, tok_count), jnp.float32),
            pltpu.VMEM((head_size, tok_count), jnp.bfloat16),
            pltpu.VMEM((tok_count, head_size), jnp.float32),
            pltpu.VMEM((tok_count, head_size), jnp.float32),
        ],
        compiler_params=params(),
        cost_estimate=pl.CostEstimate(
            flops=10 * tok_count * tok_count * q_width,
            bytes_accessed=6 * tok_count * q_width + 4 * tok_count * pairs.shape[1],
            transcendentals=tok_count * tok_count * q_width // head_size,
        ),
        name="attend",
    )(queries, out_grad, pairs, seg_row.reshape(-1, 1), seg_row, cos_tab, sin_tab)


def parts_kernel(group, block_of, used, tok_ref, pair_ref, out_ref):
    step = pl.program_id(0)
    for r in range(group):
        slot = step * group + r
        rows = slice(r * BR, (r + 1) * BR)

        @pl.when(used[slot] != 0)
        def _():
            cols = pl.ds(pl.multiple_of(block_of[slot] * BR, BR), BR)
            out_ref[rows, :] = lax.dot_general(
                tok_ref[:, cols], pair_ref[...], (((0,), (0,)), ((), ())),
                preferred_element_type=jnp.float32,
            ).astype(jnp.bfloat16)

        @pl.when(used[slot] == 0)
        def _():
            out_ref[rows, :] = jnp.zeros((BR, out_ref.shape[1]), jnp.bfloat16)


def slot_parts(tokens, pairs, block_of, used):
    slot_total = block_of.shape[0]
    group = group_of(slot_total)
    width = pairs.shape[1]
    return pl.pallas_call(
        functools.partial(parts_kernel, group),
        out_shape=jax.ShapeDtypeStruct((slot_total * BR, width), jnp.bfloat16),
        grid_spec=pltpu.PrefetchScalarGridSpec(
            num_scalar_prefetch=2,
            grid=(slot_total // group,),
            in_specs=[
                pl.BlockSpec(tokens.shape, lambda i, b, u: (0, 0)),
                pl.BlockSpec(pairs.shape, lambda i, b, u: (0, 0)),
            ],
            out_specs=pl.BlockSpec((group * BR, width), lambda i, b, u: (i, 0)),
        ),
        compiler_params=params(),
        cost_estimate=pl.CostEstimate(
            flops=2 * tokens.size * width,
            bytes_accessed=2 * (tokens.size + slot_total * BR * width),
            transcendentals=0,
        ),
        name="slot_parts",
    )(block_of, used, tokens, pairs)


def input_kernel(group, add, place, pair_ref, *refs):
    blocks, out_ref = refs[:group], refs[-1]
    w = jnp.concatenate([b[...] for b in blocks], axis=0)
    total = lax.dot_general(
        pair_ref[...], w, (((1,), (1,)), ((), ())), preferred_element_type=jnp.float32
    )
    if add:
        total = total + refs[group][...].astype(jnp.float32)
    out_ref[...] = total.astype(jnp.bfloat16)


def input_part(pairs, gathered, place, other=None):
    tok_count, width = pairs.shape
    count = place.shape[0]
    group = group_of(count)
    wide = pl.BlockSpec((tok_count, group * BR), lambda i, p: (0, i))
    add = other is not None
    return pl.pallas_call(
        functools.partial(input_kernel, group, add),
        out_shape=jax.ShapeDtypeStruct((tok_count, count * BR), jnp.bfloat16),
        grid_spec=pltpu.PrefetchScalarGridSpec(
            num_scalar_prefetch=1,
            grid=(count // group,),
            in_specs=[pl.BlockSpec(pairs.shape, lambda i, p: (0, 0))]
            + block_specs(group, width)
            + ([wide] if add else []),
            out_specs=wide,
        ),
        compiler_params=params(),
        cost_estimate=pl.CostEstimate(
            flops=2 * tok_count * width * count * BR,
            bytes_accessed=2 * (count * BR * width + 2 * tok_count * count * BR),
            transcendentals=0,
        ),
        name="input_own" if add else "input_other",
    )(place, pairs, *([gathered] * group), *((other,) if add else ()))


def local(tokens, queries, out_grad, segment_ids, weight_slots, old_place, new_place):
    tok_count = tokens.shape[0]
    slot_rows, head_count, _, head_size = weight_slots.shape
    width = head_count * 2 * head_size
    dp_count = lax.axis_size("dp")
    mp_count = lax.axis_size("mp")
    slot_total = dp_count * (slot_rows // BR)
    block_count = old_place.shape[0]

    gathered = lax.all_gather(weight_slots.reshape(slot_rows, width), "dp", axis=0, tiled=True)

    half = head_size // 2
    frequency = 500000.0 ** (-2.0 * jnp.arange(half, dtype=jnp.float32) / head_size)
    angle = jnp.arange(tok_count, dtype=jnp.float32)[:, None] * frequency[None, :]
    cos_half, sin_half = jnp.cos(angle), jnp.sin(angle)
    cos_tab = jnp.concatenate([cos_half, cos_half], axis=1)
    sin_tab = jnp.concatenate([-sin_half, sin_half], axis=1)

    pairs = project(tokens, gathered, old_place, cos_tab, sin_tab, head_size)
    query_grad, pair_grad = attend(
        queries.reshape(tok_count, -1), out_grad.reshape(tok_count, -1), pairs, segment_ids,
        cos_tab, sin_tab, head_count, head_size,
    )

    slot_ids = jnp.arange(slot_total, dtype=jnp.int32)
    matched = (new_place[None, :] == slot_ids[:, None]).astype(jnp.int32)
    block_of = jnp.sum(matched * jnp.arange(block_count, dtype=jnp.int32)[None, :], axis=1)
    used = jnp.sum(matched, axis=1)
    term = slot_parts(tokens, pair_grad, block_of, used)
    term, pair_later, query_grad = lax.optimization_barrier((term, pair_grad, query_grad))
    weight_grad = lax.psum_scatter(term, "dp", scatter_dimension=0, tiled=True)

    me = lax.axis_index("mp")
    share = old_place.reshape(mp_count, block_count // mp_count)
    total = None
    for gap in range(1, mp_count):
        target = lax.rem(me + gap, mp_count)
        places = lax.dynamic_index_in_dim(share, target, 0, keepdims=False)
        piece = input_part(pair_later, gathered, places)
        ring = [(i, (i + gap) % mp_count) for i in range(mp_count)]
        arrived = lax.ppermute(piece, "mp", ring)
        total = arrived if total is None else total + arrived
    mine = lax.dynamic_index_in_dim(share, me, 0, keepdims=False)
    input_grad = input_part(pair_later, gathered, mine, total)
    return (
        input_grad,
        query_grad.reshape(queries.shape),
        weight_grad.astype(jnp.float32).reshape(slot_rows, head_count, 2, head_size),
    )


def solution(mesh):
    return jax.shard_map(
        local,
        mesh=mesh,
        in_specs=(
            P("dp", None),
            P("dp", "mp", None),
            P("dp", "mp", None),
            P("dp", None),
            P("dp", "mp", None, None),
            P(),
            P(),
        ),
        out_specs=(P("dp", "mp"), P("dp", "mp", None), P("dp", "mp", None, None)),
        check_vma=False,
    )
```

profile of v0, /device:TPU:11, one launch (start us, length us, event | category | flops | bytes accessed | tf_op | source)
XLA Modules:
  0.0 614.8 jit_solution(4793941145907442811)
XLA Ops:
  7.2 0.0 copy-start
  7.2 0.0 copy-start.2
  7.2 0.0 all-gather.2.cloned.1.call-start
  7.2 4.4 reshape.39
  11.7 0.0 all-gather.2.cloned.1.call-update
  11.7 0.0 reduce-scatter.2.cloned.1.call-start
  11.7 0.0 copy-done
  11.7 0.9 copy.11.col_ref
  12.6 0.0 copy-done.2
  12.6 0.7 convert_reduce_fusion
  13.3 1.0 fusion.2
  14.3 1.0 pad_maximum_fusion
  15.3 13.2 %copy_bitcast_fusion = (bf16[512,4096]{1,0:T(8,128)(2,1)}, bf16[512,4096]{1,0:T(8,128)(2,1)}) fusion(bf16[64,8,32,128]{3,2,1,0:T(8,128)(2,1)} %bitcast.15, bf16[64,8,32,128]{3,2,1,0:T(8,128)(2,1)} %bitcast.16), kind=kLoop, calls=%fused_computation | loop fusion | bytes 16777216 | tf_op jit(solution)/shard_map/reshape | solution.py:269
  28.5 152.5 %all-gather.2.cloned.1.call-done.refs_0_.refs_1_.refs_2_.refs_3_.refs_4_.refs_5_.refs_6_.refs_7_ = bf16[16384,1024]{1,0:T(8,128)(2,1)} async-done(((bf16[1024,1024]{1,0:T(8,128)(2,1)}), bf16[16384,1024]{1,0:T(8,128)(2,1)}) %all-gather.2.cloned.1.call-update) | async-done | bytes 33554448 | tf_op jit(solution)/shard_map/all_gather | solution.py:258
  181.1 16.8 %project.1.kv_ref = bf16[512,1024]{1,0:T(8,128)(2,1)} custom-call(s32[64]{0:T(128)} %place.1, bf16[512,8192]{1,0:T(8,128)(2,1)} %tok_ref.3, f32[512,128]{1,0:T(8,128)} %get-tuple-element.20.cos_ref, f32[512,128]{1,0:T(8,128)} %get-tuple-element.21.sin_ref, ...), custom_call_target="tpu_custom_call" | custom-call | flops 8589934592 | bytes 26214400 | tf_op jit(solution)/shard_map/project/pallas_call | solution.py:63
  197.8 42.7 %attend.1 = (bf16[512,4096]{1,0:T(8,128)(2,1)}, bf16[512,1024]{1,0:T(8,128)(2,1)}) custom-call(bf16[512,4096]{1,0:T(8,128)(2,1)} %get-tuple-element.23.q_ref, bf16[512,4096]{1,0:T(8,128)(2,1)} %get-tuple-element.22.og_ref, bf16[512,1024]{1,0:T(8,128)(2,1)} %project.1.kv_ref, s32[512,1]{1,0:T(8,128)} %copy.11.col_ref, s32[1,512]{1,0:T(1,128)} %row_ref.1, ...), custom_call_target="tpu_custom_call" | custom-call | flops 10737418240 | bytes 14680064 | tf_op jit(solution)/shard_map/attend/pallas_call | solution.py:141
  240.5 31.6 %slot_parts.1 = bf16[16384,1024]{1,0:T(8,128)(2,1)} custom-call(s32[128]{0:T(128)} %get-tuple-element.14.block_of, s32[128]{0:T(128)} %get-tuple-element.13.used, bf16[512,8192]{1,0:T(8,128)(2,1)} %tok_ref.3, bf16[512,1024]{1,0:T(8,128)(2,1)} %get-tuple-element.10.pair_ref), custom_call_target="tpu_custom_call" | custom-call | flops 8589934592 | bytes 41943040 | tf_op jit(solution)/shard_map/slot_parts/pallas_call | solution.py:189
  272.1 0.0 copy-start.1
  272.1 0.0 reduce-scatter.2.cloned.1.call-update
  272.2 0.6 copy-done.1
  272.8 0.1 reshape.36
  272.9 0.5 dynamic-slice_bitcast_fusion
  273.4 10.0 %input_other.1 = bf16[512,4096]{1,0:T(8,128)(2,1)} custom-call(s32[32]{0:T(128)} %get-tuple-element.15.place, bf16[512,1024]{1,0:T(8,128)(2,1)} %get-tuple-element.10.pair_ref, bf16[16384,1024]{1,0:T(8,128)(2,1)} %all-gather.2.cloned.1.call-done.refs_0_.refs_1_.refs_2_.refs_3_.refs_4_.refs_5_.refs_6_.refs_7_, ...), custom_call_target="tpu_custom_call" | custom-call | flops 4294967296 | bytes 16777216 | tf_op jit(solution)/shard_map/input_other/pallas_call | solution.py:228
  283.4 1.2 collective-permute-start
  284.6 6.5 %copy.14 = bf16[64,8,32,128]{3,2,1,0:T(8,128)(2,1)} copy(bf16[64,8,32,128]{3,1,2,0:T(8,128)(2,1)} %bitcast.13) | data formatting | bytes 8388608
  291.1 84.4 %collective-permute-done.refs_8_ = bf16[512,4096]{1,0:T(8,128)(2,1)} collective-permute-done((bf16[512,4096]{1,0:T(8,128)(2,1)}, bf16[512,4096]{1,0:T(8,128)(2,1)}, u32[]{:S(2)}, u32[]{:S(2)}) %collective-permute-start) | collective-permute-done | bytes 4194336 | tf_op jit(solution)/shard_map/ppermute | solution.py:289
  375.5 10.7 %input_own.1 = bf16[512,4096]{1,0:T(8,128)(2,1)} custom-call(s32[32]{0:T(128)} %get-tuple-element.16.place, bf16[512,1024]{1,0:T(8,128)(2,1)} %get-tuple-element.10.pair_ref, bf16[16384,1024]{1,0:T(8,128)(2,1)} %all-gather.2.cloned.1.call-done.refs_0_.refs_1_.refs_2_.refs_3_.refs_4_.refs_5_.refs_6_.refs_7_, ...), custom_call_target="tpu_custom_call" | custom-call | flops 4294967296 | bytes 16777216 | tf_op jit(solution)/shard_map/input_own/pallas_call | solution.py:228
  386.2 215.1 %reduce-scatter.2.cloned.1.call-done = bf16[1024,1024]{1,0:T(8,128)(2,1)} async-done(((bf16[16384,1024]{1,0:T(8,128)(2,1)}), bf16[1024,1024]{1,0:T(8,128)(2,1)}) %reduce-scatter.2.cloned.1.call-update) | async-done | bytes 2097168 | tf_op jit(solution)/shard_map/reduce_scatter | solution.py:279
  601.4 6.6 %reshape.45 = f32[1024,4,2,128]{3,2,1,0:T(2,128)} reshape(bf16[1024,1024]{1,0:T(8,128)(2,1)} %reduce-scatter.2.cloned.1.call-done) | data formatting | bytes 6291456 | tf_op jit(solution)/shard_map/reshape | solution.py:296
  (1 shorter events, 0.0 us)
Async XLA Ops:
  7.2 4.6 copy-start
  7.2 5.4 copy-start.2
  7.2 173.9 %all-gather.2.cloned.1.call-start = ((), (), s32[]{:S(2)}) async-start(), calls=%async_computation.1 | async-start | bytes 35651584 | tf_op jit(solution)/shard_map/all_gather | solution.py:258
  11.7 589.7 %reduce-scatter.2.cloned.1.call-start = ((), (), s32[]{:S(2)}) async-start(), calls=%async_computation.2 | async-start | bytes 35651584 | tf_op jit(solution)/shard_map/reduce_scatter | solution.py:279
  272.1 0.7 copy-start.1
  283.4 92.1 %collective-permute-start = (bf16[512,4096]{1,0:T(8,128)(2,1)}, bf16[512,4096]{1,0:T(8,128)(2,1)}, u32[]{:S(2)}, u32[]{:S(2)}) collective-permute-start(bf16[512,4096]{1,0:T(8,128)(2,1)} %input_other.1), channel_id=1, source_target_pairs={{0,1},{1,0},{2,3},{3,2},{4,5},{5,4},{6,7},{7,6},{8,9},{9,8},{10,11... | collective-permute-start | bytes 12582920 | tf_op jit(solution)/shard_map/ppermute | solution.py:289
Sparse Core Ops, SparseCore 0:
  11.8 169.2 all-gather.1
  272.3 329.0 reduce-scatter.1
where the time goes:
time: 618 us; the launch traced here: 615 us
  waiting for transfers between devices  452 us (73%)
  Pallas kernels  112 us (18%)
  local copies, waits for them, and re-layouts  32.8 us (5%)
  between operations  14.1 us (2%)
    reduce_scatter x1, waiting for transfers between devices, local(): weight_grad = lax.psum_scatter(term, 'dp', scatter_dimension=0, tiled=True)  215 us
    all_gather x1, waiting for transfers between devices, local(): lax.all_gather(weight_slots.reshape(slot_rows, width), 'dp', axis=0, tile...  153 us
    ppermute x1, waiting for transfers between devices, local(): arrived = lax.ppermute(piece, 'mp', ring)  84.4 us
    pallas_call x1, Pallas kernels, attend(): pl.pallas_call(functools.partial(attend_kernel, per_head, tile), out_shap...  42.7 us
    pallas_call x1, Pallas kernels, slot_parts(): pl.pallas_call(functools.partial(parts_kernel, group), out_shape=jax.Shap...  31.6 us
    pallas_call x2, Pallas kernels, input_part(): pl.pallas_call(functools.partial(input_kernel, group, add), out_shape=jax...  20.7 us
    pallas_call x1, Pallas kernels, project(): pl.pallas_call(functools.partial(project_kernel, group, head_size), out_s...  16.8 us
    reshape x1, local copies, waits for them, and re-layouts, local(): out_grad.reshape(tok_count, -1)  13.2 us
  transfers between devices with their start and end apart: 3, of which 3 were waited for; matrix products, arithmetic and copies ran while one was open for 4% of the time, Pallas kernels for 3%

commit v1 on v0

--- a/solution.py
+++ b/solution.py
@@ -10,6 +10,7 @@
 BR = 128
 LOG2E = 1.4426950408889634
 VMEM_LIMIT = 60 * 1024 * 1024
+MESH = pl.DeviceIdType.MESH
 
 
 def params():
@@ -163,49 +164,186 @@
     )(queries, out_grad, pairs, seg_row.reshape(-1, 1), seg_row, cos_tab, sin_tab)
 
 
-def parts_kernel(group, block_of, used, tok_ref, pair_ref, out_ref):
-    step = pl.program_id(0)
-    for r in range(group):
-        slot = step * group + r
-        rows = slice(r * BR, (r + 1) * BR)
-
-        @pl.when(used[slot] != 0)
-        def _():
-            cols = pl.ds(pl.multiple_of(block_of[slot] * BR, BR), BR)
-            out_ref[rows, :] = lax.dot_general(
-                tok_ref[:, cols], pair_ref[...], (((0,), (0,)), ((), ())),
-                preferred_element_type=jnp.float32,
-            ).astype(jnp.bfloat16)
-
-        @pl.when(used[slot] == 0)
-        def _():
-            out_ref[rows, :] = jnp.zeros((BR, out_ref.shape[1]), jnp.bfloat16)
-
-
-def slot_parts(tokens, pairs, block_of, used):
-    slot_total = block_of.shape[0]
-    group = group_of(slot_total)
+def chip_at(chips, position):
+    return jnp.where(position < chips // 2, 2 * position, 2 * (chips - 1 - position) + 1)
+
+
+def scatter_kernel(
+    chips, subs, block_of, used, tok_ref, pair_ref, out_ref,
+    part_out, part_in, ring_out, ring_in, final, swap_out, swap_in,
+    part_sent, part_got, ring_sent, ring_got, swap_sent, swap_got,
+):
+    dp_count = 2 * chips
+    me = lax.axis_index("dp")
+    chip, core = me // 2, lax.rem(me, 2)
+    half = chip // 2
+    place = jnp.where(lax.rem(chip, 2) == 0, half, chips - 1 - half)
+    ahead = 2 * chip_at(chips, lax.rem(place + 1, chips)) + core
+    behind = 2 * chip_at(chips, lax.rem(place + chips - 1, chips)) + core
+    partner = 2 * chip + 1 - core
+    piece_rows, tok_count = tok_ref.shape[1:]
+    cols = pair_ref.shape[1] // 2
+    sub = piece_rows // subs
+    slots, short = swap_out.shape[1:3]
+
+    barrier = pltpu.get_barrier_semaphore()
+
+    @pl.loop(1, dp_count)
+    def _(k):
+        pl.semaphore_signal(
+            barrier, inc=1, device_id={"dp": lax.rem(me + k, dp_count)}, device_id_type=MESH
+        )
+
+    pl.semaphore_wait(barrier, dp_count - 1)
+
+    def goal(way, step):
+        offset = chips - 1 - step if way == 0 else 1 + step
+        return chip_at(chips, lax.rem(place + offset, chips))
+
+    def product(piece, rows, way):
+        return jnp.dot(
+            tok_ref[piece, rows, :], pair_ref[:, way * cols : (way + 1) * cols],
+            preferred_element_type=jnp.float32,
+        )
+
+    def part_copy(way, step):
+        return pltpu.make_async_remote_copy(
+            src_ref=part_out.at[way, step], dst_ref=part_in.at[way, step],
+            send_sem=part_sent.at[way, step], recv_sem=part_got.at[way, step],
+            device_id={"dp": partner}, device_id_type=MESH,
+        )
+
+    def ring_copy(way, step, u):
+        rows = pl.ds(u * sub, sub)
+        return pltpu.make_async_remote_copy(
+            src_ref=ring_out.at[way, step, rows], dst_ref=ring_in.at[way, step, rows],
+            send_sem=ring_sent.at[way, step, u], recv_sem=ring_got.at[way, step, u],
+            device_id={"dp": ahead if way == 0 else behind}, device_id_type=MESH,
+        )
+
+    def send_part(step):
+        for way in range(2):
+            piece = 2 * goal(way, step) + 1 - core
+            for u in range(subs):
+                rows = slice(u * sub, (u + 1) * sub)
+                part_out[way, step, rows, :] = product(piece, rows, way).astype(jnp.bfloat16)
+            part_copy(way, step).start()
+
+    def ring_step(step, first, last):
+        for way in range(2):
+            part_copy(way, step).wait_recv()
+        for u in range(subs):
+            rows = slice(u * sub, (u + 1) * sub)
+            for way in range(2):
+                piece = 2 * goal(way, step) + core
+                total = product(piece, rows, way) + part_in[way, step, rows, :].astype(jnp.float32)
+                if not first:
+                    ring_copy(way, step - 1, u).wait_recv()
+                    total = total + ring_in[way, step - 1, rows, :].astype(jnp.float32)
+                if last:
+                    blocks = pl.ds(u * (sub // short), sub // short)
+                    final[blocks, :, way * cols : (way + 1) * cols] = total.reshape(
+                        sub // short, short, cols
+                    ).astype(jnp.bfloat16)
+                else:
+                    ring_out[way, step, rows, :] = total.astype(jnp.bfloat16)
+                    ring_copy(way, step, u).start()
+
+    send_part(0)
+    send_part(1)
+    ring_step(0, True, False)
+
+    @pl.loop(1, chips - 1)
+    def _(step):
+        send_part(step + 1)
+        ring_step(step, False, False)
+
+    ring_step(chips - 1, False, True)
+
+    def swap_copy(k):
+        peer = lax.rem(me + k, dp_count)
+        return pltpu.make_async_remote_copy(
+            src_ref=swap_out.at[peer], dst_ref=swap_in.at[me],
+            send_sem=swap_sent.at[k], recv_sem=swap_got.at[k],
+            device_id={"dp": peer}, device_id_type=MESH,
+        )
+
+    def fill(peer):
+        for i in range(slots):
+            slot = peer * slots + i
+            rows = final[block_of[slot]]
+            swap_out[peer, i] = jnp.where(used[slot] != 0, rows, jnp.zeros_like(rows))
+
+    @pl.loop(1, dp_count)
+    def _(k):
+        fill(lax.rem(me + k, dp_count))
+        swap_copy(k).start()
+
+    fill(me)
+    out_ref[:, pl.ds(me, 1)] = swap_out[me].astype(jnp.float32)[:, None]
+
+    @pl.loop(1, dp_count)
+    def _(k):
+        swap_copy(k).wait_recv()
+        origin = lax.rem(me + dp_count - k, dp_count)
+        out_ref[:, pl.ds(origin, 1)] = swap_in[origin].astype(jnp.float32)[:, None]
+
+    @pl.loop(1, dp_count)
+    def _(k):
+        swap_copy(k).wait_send()
+
+    @pl.loop(0, chips)
+    def _(step):
+        for way in range(2):
+            part_copy(way, step).wait_send()
+
+    @pl.loop(0, chips - 1)
+    def _(step):
+        for way in range(2):
+            for u in range(subs):
+                ring_copy(way, step, u).wait_send()
+
+
+def scatter_sum(tok_pieces, pairs, block_of, used, dp_count):
+    chips = dp_count // 2
     width = pairs.shape[1]
+    piece_rows = tok_pieces.shape[1]
+    slots = block_of.shape[0] // dp_count
+    short = BR // dp_count
+    subs = 4
+    whole = pl.BlockSpec(memory_space=pltpu.VMEM)
+    scalars = pl.BlockSpec(memory_space=pltpu.SMEM)
+    cols = width // 2
+    bf = jnp.bfloat16
+    sent = 2 * 2 * (chips - 1) * piece_rows * cols * 2
     return pl.pallas_call(
-        functools.partial(parts_kernel, group),
-        out_shape=jax.ShapeDtypeStruct((slot_total * BR, width), jnp.bfloat16),
-        grid_spec=pltpu.PrefetchScalarGridSpec(
-            num_scalar_prefetch=2,
-            grid=(slot_total // group,),
-            in_specs=[
-                pl.BlockSpec(tokens.shape, lambda i, b, u: (0, 0)),
-                pl.BlockSpec(pairs.shape, lambda i, b, u: (0, 0)),
-            ],
-            out_specs=pl.BlockSpec((group * BR, width), lambda i, b, u: (i, 0)),
-        ),
-        compiler_params=params(),
+        functools.partial(scatter_kernel, chips, subs),
+        out_shape=jax.ShapeDtypeStruct((slots, dp_count, short, width), jnp.float32),
+        in_specs=[scalars, scalars, whole, whole],
+        out_specs=whole,
+        scratch_shapes=[
+            pltpu.VMEM((2, chips, piece_rows, cols), bf),
+            pltpu.VMEM((2, chips, piece_rows, cols), bf),
+            pltpu.VMEM((2, chips - 1, piece_rows, cols), bf),
+            pltpu.VMEM((2, chips - 1, piece_rows, cols), bf),
+            pltpu.VMEM((piece_rows // short, short, width), bf),
+            pltpu.VMEM((dp_count, slots, short, width), bf),
+            pltpu.VMEM((dp_count, slots, short, width), bf),
+            pltpu.SemaphoreType.DMA((2, chips)),
+            pltpu.SemaphoreType.DMA((2, chips)),
+            pltpu.SemaphoreType.DMA((2, chips - 1, subs)),
+            pltpu.SemaphoreType.DMA((2, chips - 1, subs)),
+            pltpu.SemaphoreType.DMA((dp_count,)),
+            pltpu.SemaphoreType.DMA((dp_count,)),
+        ],
+        compiler_params=pltpu.CompilerParams(
+            collective_id=0, has_side_effects=True, vmem_limit_bytes=VMEM_LIMIT
+        ),
         cost_estimate=pl.CostEstimate(
-            flops=2 * tokens.size * width,
-            bytes_accessed=2 * (tokens.size + slot_total * BR * width),
-            transcendentals=0,
-        ),
-        name="slot_parts",
-    )(block_of, used, tokens, pairs)
+            flops=2 * tok_pieces.size * width * 8, bytes_accessed=sent, transcendentals=0
+        ),
+        name="scatter_sum",
+    )(block_of, used, tok_pieces, pairs)
 
 
 def input_kernel(group, add, place, pair_ref, *refs):
@@ -274,9 +412,9 @@
     matched = (new_place[None, :] == slot_ids[:, None]).astype(jnp.int32)
     block_of = jnp.sum(matched * jnp.arange(block_count, dtype=jnp.int32)[None, :], axis=1)
     used = jnp.sum(matched, axis=1)
-    term = slot_parts(tokens, pair_grad, block_of, used)
-    term, pair_later, query_grad = lax.optimization_barrier((term, pair_grad, query_grad))
-    weight_grad = lax.psum_scatter(term, "dp", scatter_dimension=0, tiled=True)
+    short = BR // dp_count
+    tok_pieces = tokens.reshape(tok_count, block_count, dp_count, short).transpose(2, 1, 3, 0)
+    tok_pieces = tok_pieces.reshape(dp_count, block_count * short, tok_count)
 
     me = lax.axis_index("mp")
     share = old_place.reshape(mp_count, block_count // mp_count)
@@ -284,16 +422,17 @@
     for gap in range(1, mp_count):
         target = lax.rem(me + gap, mp_count)
         places = lax.dynamic_index_in_dim(share, target, 0, keepdims=False)
-        piece = input_part(pair_later, gathered, places)
+        piece = input_part(pair_grad, gathered, places)
         ring = [(i, (i + gap) % mp_count) for i in range(mp_count)]
         arrived = lax.ppermute(piece, "mp", ring)
         total = arrived if total is None else total + arrived
+    weight_grad = scatter_sum(tok_pieces, pair_grad, block_of, used, dp_count)
     mine = lax.dynamic_index_in_dim(share, me, 0, keepdims=False)
-    input_grad = input_part(pair_later, gathered, mine, total)
+    input_grad = input_part(pair_grad, gathered, mine, total)
     return (
         input_grad,
         query_grad.reshape(queries.shape),
-        weight_grad.astype(jnp.float32).reshape(slot_rows, head_count, 2, head_size),
+        weight_grad.reshape(slot_rows, head_count, 2, head_size),
     )
 
 

time: 618 us -> 423 us (0.68)
  waiting for transfers between devices: 452 us -> 132 us
  Pallas kernels: 112 us -> 221 us
  local copies, waits for them, and re-layouts: 32.8 us -> 50.9 us
    reduce_scatter x1 -> x0, waiting for transfers between devices: 215 us -> none  [local(): weight_grad = lax.psum_scatter(term, 'dp', scatter_dimension=0, tiled=True)]
    pallas_call x1, Pallas kernels: 31.6 us -> 141 us  [scatter_sum(): pl.pallas_call(functools.partial(scatter_kernel, chips, subs), out_shape=...]
    ppermute x1, waiting for transfers between devices: 84.4 us -> 0.01 us  [local(): arrived = lax.ppermute(piece, 'mp', ring)]
    all_gather x1, waiting for transfers between devices: 153 us -> 132 us  [local(): lax.all_gather(weight_slots.reshape(slot_rows, width), 'dp', axis=0, tile...]
    unnamed x7 -> x8, local copies, waits for them, and re-layouts: 7.12 us -> 17.5 us
    transpose x0 -> x1, local copies, waits for them, and re-layouts: none -> 7.63 us  [local(): tokens.reshape(tok_count, block_count, dp_count, short)]
  transfers between devices with their start and end apart: 3 -> 2, of which waited for: 3 -> 1; matrix products, arithmetic and copies ran while one was open for 4% -> 12% of each run, Pallas kernels for 3% -> 33%
where the time goes in v1:
time: 423 us
  Pallas kernels  221 us (52%)
  waiting for transfers between devices  132 us (31%)
  local copies, waits for them, and re-layouts  50.9 us (12%)
  between operations  14.1 us (3%)
    pallas_call x1, Pallas kernels, scatter_sum(): pl.pallas_call(functools.partial(scatter_kernel, chips, subs), out_shape=...  141 us
    all_gather x1, waiting for transfers between devices, local(): lax.all_gather(weight_slots.reshape(slot_rows, width), 'dp', axis=0, tile...  132 us
    pallas_call x1, Pallas kernels, attend(): pl.pallas_call(functools.partial(attend_kernel, per_head, tile), out_shap...  42.6 us
    pallas_call x2, Pallas kernels, input_part(): pl.pallas_call(functools.partial(input_kernel, group, add), out_shape=jax...  20.7 us
    unnamed x8, local copies, waits for them, and re-layouts  17.5 us
    pallas_call x1, Pallas kernels, project(): pl.pallas_call(functools.partial(project_kernel, group, head_size), out_s...  16.8 us
    reshape x1, local copies, waits for them, and re-layouts, local(): out_grad.reshape(tok_count, -1)  13.2 us
  transfers between devices with their start and end apart: 2, of which 1 were waited for; matrix products, arithmetic and copies ran while one was open for 12% of the time, Pallas kernels for 33%

profile of v1, /device:TPU:11, one launch (start us, length us, event | category | flops | bytes accessed | tf_op | source)
XLA Modules:
  0.0 422.6 jit_solution(17151188150272656127)
XLA Ops:
  7.2 0.0 copy-start.1
  7.2 0.0 copy-start
  7.2 0.0 all-gather.2.cloned.1.call-start
  7.2 4.4 %reshape.42 = bf16[1024,1024]{1,0:T(8,128)(2,1)} reshape(bf16[1024,4,2,128]{3,2,1,0:T(2,128)(2,1)} %param.11) | data formatting | bytes 4194304 | tf_op jit(solution)/shard_map/reshape | solution.py:396
  11.7 0.0 all-gather.2.cloned.1.call-update
  11.7 0.0 copy-done.1
  11.7 0.1 reshape.39
  11.8 0.0 copy-done
  11.8 0.8 copy.14.col_ref
  12.6 12.0 %copy.15 = bf16[512,8192]{0,1:T(8,128)(2,1)} copy(bf16[512,8192]{1,0:T(8,128)(2,1)} %tok_ref.1) | data formatting | bytes 16777216 | tf_op args[0]
  24.7 0.0 copy-start.2
  24.7 7.6 %copy.23 = bf16[16,64,8,512]{3,2,1,0:T(8,128)(2,1)} copy(bf16[16,64,8,512]{3,2,0,1:T(8,128)(2,1)} %bitcast.21) | data formatting | bytes 16777216 | tf_op jit(solution)/shard_map/transpose | solution.py:416
  32.3 0.6 dynamic-slice_bitcast_fusion
  32.9 0.0 copy-done.2
  32.9 0.7 convert_reduce_fusion
  33.6 1.0 fusion.2
  34.6 1.0 pad_maximum_fusion
  35.6 13.2 %copy_bitcast_fusion.1 = (bf16[512,4096]{1,0:T(8,128)(2,1)}, bf16[512,4096]{1,0:T(8,128)(2,1)}) fusion(bf16[64,8,32,128]{3,2,1,0:T(8,128)(2,1)} %bitcast.25, bf16[64,8,32,128]{3,2,1,0:T(8,128)(2,1)} %bitcast.26), kind=kLoop, calls=%fused_computation.1 | loop fusion | bytes 16777216 | tf_op jit(solution)/shard_map/reshape | solution.py:407
  48.8 132.3 %all-gather.2.cloned.1.call-done.refs_0_.refs_1_.refs_2_.refs_3_.refs_4_.refs_5_.refs_6_.refs_7_ = bf16[16384,1024]{1,0:T(8,128)(2,1)} async-done(((bf16[1024,1024]{1,0:T(8,128)(2,1)}), bf16[16384,1024]{1,0:T(8,128)(2,1)}) %all-gather.2.cloned.1.call-update) | async-done | bytes 33554448 | tf_op jit(solution)/shard_map/all_gather | solution.py:396
  181.1 16.8 %project.1.kv_ref = bf16[512,1024]{1,0:T(8,128)(2,1)} custom-call(s32[64]{0:T(128)} %place.1, bf16[512,8192]{1,0:T(8,128)(2,1)} %tok_ref.1, f32[512,128]{1,0:T(8,128)} %get-tuple-element.14.cos_ref, f32[512,128]{1,0:T(8,128)} %get-tuple-element.15.sin_ref, ...), custom_call_target="tpu_custom_call" | custom-call | flops 8589934592 | bytes 26214400 | tf_op jit(solution)/shard_map/project/pallas_call | solution.py:64
  197.8 42.6 %attend.1 = (bf16[512,4096]{1,0:T(8,128)(2,1)}, bf16[512,1024]{1,0:T(8,128)(2,1)}) custom-call(bf16[512,4096]{1,0:T(8,128)(2,1)} %get-tuple-element.17.q_ref, bf16[512,4096]{1,0:T(8,128)(2,1)} %get-tuple-element.16.og_ref, bf16[512,1024]{1,0:T(8,128)(2,1)} %project.1.kv_ref, s32[512,1]{1,0:T(8,128)} %copy.14.col_ref, s32[1,512]{1,0:T(1,128)} %row_ref.1, ...), custom_call_target="tpu_custom_call" | custom-call | flops 10737418240 | bytes 14680064 | tf_op jit(solution)/shard_map/attend/pallas_call | solution.py:142
  240.5 10.1 %input_other.1 = bf16[512,4096]{1,0:T(8,128)(2,1)} custom-call(s32[32]{0:T(128)} %get-tuple-element.9.place, bf16[512,1024]{1,0:T(8,128)(2,1)} %get-tuple-element.5.pair_ref, bf16[16384,1024]{1,0:T(8,128)(2,1)} %all-gather.2.cloned.1.call-done.refs_0_.refs_1_.refs_2_.refs_3_.refs_4_.refs_5_.refs_6_.refs_7_, ...), custom_call_target="tpu_custom_call" | custom-call | flops 4294967296 | bytes 16777216 | tf_op jit(solution)/shard_map/input_other/pallas_call | solution.py:366
  250.5 1.2 collective-permute-start
  251.7 141.4 %scatter_sum.1 = f32[8,16,8,1024]{3,2,1,0:T(8,128)} custom-call(s32[128]{0:T(128)} %get-tuple-element.8.block_of, s32[128]{0:T(128)} %get-tuple-element.7.used, bf16[16,512,512]{2,1,0:T(8,128)(2,1)} %bitcast.22, bf16[512,1024]{1,0:T(8,128)(2,1)} %get-tuple-element.5.pair_ref), custom_call_target="tpu_custom_call" | custom-call | flops 68719476736 | bytes 14680064 | tf_op jit(solution)/shard_map/scatter_sum/pallas_call | solution.py:319
  393.1 6.6 %reshape.47 = f32[1024,4,2,128]{3,2,1,0:T(2,128)} reshape(f32[8,16,8,1024]{3,2,1,0:T(8,128)} %scatter_sum.1) | data formatting | bytes 8388608 | tf_op jit(solution)/shard_map/reshape | solution.py:435
  399.7 5.5 %copy.19 = bf16[64,8,32,128]{3,2,1,0:T(8,128)(2,1)} copy(bf16[64,8,32,128]{3,1,2,0:T(8,128)(2,1)} %bitcast.23) | data formatting | bytes 8388608
  405.2 0.0 collective-permute-done.refs_8_
  405.2 10.6 %input_own.1 = bf16[512,4096]{1,0:T(8,128)(2,1)} custom-call(s32[32]{0:T(128)} %get-tuple-element.10.place, bf16[512,1024]{1,0:T(8,128)(2,1)} %get-tuple-element.5.pair_ref, bf16[16384,1024]{1,0:T(8,128)(2,1)} %all-gather.2.cloned.1.call-done.refs_0_.refs_1_.refs_2_.refs_3_.refs_4_.refs_5_.refs_6_.refs_7_, ...), custom_call_target="tpu_custom_call" | custom-call | flops 4294967296 | bytes 16777216 | tf_op jit(solution)/shard_map/input_own/pallas_call | solution.py:366
  (1 shorter events, 0.0 us)
Async XLA Ops:
  7.2 4.5 %copy-start.1 = (s32[64]{0:T(128)S(1)}, s32[64]{0:T(128)}, u32[]{:S(2)}) copy-start(s32[64]{0:T(128)} %place.1) | copy-start | bytes 772
  7.2 4.6 %copy-start = (s32[1,512]{1,0:T(1,128)S(1)}, s32[1,512]{1,0:T(1,128)}, u32[]{:S(2)}) copy-start(s32[1,512]{1,0:T(1,128)} %row_ref.1) | copy-start | bytes 6148
  7.2 173.9 %all-gather.2.cloned.1.call-start = ((), (), s32[]{:S(2)}) async-start(), calls=%async_computation | async-start | bytes 35651584 | tf_op jit(solution)/shard_map/all_gather | solution.py:396
  24.7 8.2 %copy-start.2 = (s32[64]{0:T(128)S(1)}, s32[64]{0:T(128)}, u32[]{:S(2)}) copy-start(s32[64]{0:T(128)} %param.13) | copy-start | bytes 772
  250.5 154.6 %collective-permute-start = (bf16[512,4096]{1,0:T(8,128)(2,1)}, bf16[512,4096]{1,0:T(8,128)(2,1)}, u32[]{:S(2)}, u32[]{:S(2)}) collective-permute-start(bf16[512,4096]{1,0:T(8,128)(2,1)} %input_other.1), channel_id=1, source_target_pairs={{0,1},{1,0},{2,3},{3,2},{4,5},{5,4},{6,7},{7,6},{8,9},{9,8},{10,11... | collective-permute-start | bytes 12582920 | tf_op jit(solution)/shard_map/ppermute | solution.py:427
Sparse Core Ops, SparseCore 0:
  11.8 169.2 all-gather.1

commit v2 on v1

v2 whole, which is shorter than its diff:
```python
import functools

import jax
import jax.numpy as jnp
from jax import lax
from jax.experimental import pallas as pl
from jax.experimental.pallas import tpu as pltpu
from jax.sharding import PartitionSpec as P

BR = 128
LOG2E = 1.4426950408889634
VMEM_LIMIT = 60 * 1024 * 1024
MESH = pl.DeviceIdType.MESH


def params():
    return pltpu.CompilerParams(
        dimension_semantics=("arbitrary",), vmem_limit_bytes=VMEM_LIMIT
    )


def group_of(count):
    for size in (8, 4, 2):
        if count % size == 0:
            return size
    return 1


def chip_at(chips, position):
    return jnp.where(position < chips // 2, 2 * position, 2 * (chips - 1 - position) + 1)


def position_of(chips, chip):
    return jnp.where(lax.rem(chip, 2) == 0, chip // 2, chips - 1 - chip // 2)


def meet(dp_count, me):
    barrier = pltpu.get_barrier_semaphore()

    @pl.loop(1, dp_count)
    def _(k):
        pl.semaphore_signal(
            barrier, inc=1, device_id={"dp": lax.rem(me + k, dp_count)}, device_id_type=MESH
        )

    pl.semaphore_wait(barrier, dp_count - 1)


def remote(src, dst, sent, got, peer):
    return pltpu.make_async_remote_copy(
        src_ref=src, dst_ref=dst, send_sem=sent, recv_sem=got,
        device_id={"dp": peer}, device_id_type=MESH,
    )


def gather_kernel(
    chips, heads, subs, tile, place, slots_ref, tok_hbm, q_hbm, og_hbm, col_ref, row_ref,
    cos_ref, sin_ref, dq_ref, pair_ref, w_hbm, tokt_hbm,
    tok, q_ref, og_ref, tokt, w, got, total, kv, bias, key_t, rot_acc, val_acc,
    load_sem, save_sem, swap_sent, swap_got, ring_sent, ring_got, pass_sent, pass_got,
):
    dp_count = 2 * chips
    hops = chips // 2
    me = lax.axis_index("dp")
    core = lax.rem(me, 2)
    spot = position_of(chips, me // 2)
    partner = me + 1 - 2 * core
    groups, blocks, splits, rows, lane = w.shape
    per = chips // groups
    slots = slots_ref.shape[0]
    tok_count, hd = tok.shape[0], lane
    per_head = q_ref.shape[1] // heads // hd
    near = (
        2 * chip_at(chips, lax.rem(spot + 1, chips)) + core,
        2 * chip_at(chips, lax.rem(spot + chips - 1, chips)) + core,
    )
    size = blocks // subs
    inv_root = 1.0 / (hd ** 0.5)

    loads = [
        pltpu.make_async_copy(src, dst, load_sem.at[i])
        for i, (src, dst) in enumerate(((tok_hbm, tok), (q_hbm, q_ref), (og_hbm, og_ref)))
    ]
    for load in loads:
        load.start()

    def part(position, owner):
        return position // per, lax.rem(position, per) * 2 + owner

    meet(dp_count, me)

    def swap_copy(k):
        peer = lax.rem(me + k, dp_count)
        group, split = part(position_of(chips, peer // 2), lax.rem(peer, 2))
        src = slots_ref.at[
            :, pl.ds(pl.multiple_of(split * rows, rows), rows),
            pl.ds(pl.multiple_of(group * lane, lane), lane),
        ]
        return remote(src, got.at[me], swap_sent.at[k], swap_got.at[k], peer)

    @pl.loop(1, dp_count)
    def _(k):
        swap_copy(k).start()

    my_group, my_split = part(spot, core)
    own_rows = pl.ds(pl.multiple_of(my_split * rows, rows), rows)
    own_lanes = pl.ds(pl.multiple_of(my_group * lane, lane), lane)
    got[me] = slots_ref[:, own_rows, own_lanes]

    kpos = lax.broadcasted_iota(jnp.int32, bias.shape, 0)
    qpos = lax.broadcasted_iota(jnp.int32, bias.shape, 1)
    allowed = (kpos <= qpos) & (col_ref[...] == row_ref[...])
    bias[...] = jnp.where(allowed, 0.0, -1e30).astype(jnp.float32)

    for load in loads:
        load.wait()

    @pl.loop(0, blocks)
    def _(b):
        cols = tok[:, pl.ds(pl.multiple_of(b * BR, BR), BR)]
        flipped = cols.astype(jnp.float32).T
        tokt[b] = flipped.reshape(splits, rows, tok_count).astype(jnp.bfloat16)

    save_tok = pltpu.make_async_copy(tokt, tokt_hbm, save_sem.at[groups])
    save_tok.start()

    @pl.loop(1, dp_count)
    def _(k):
        swap_copy(k).wait_recv()

    def piece(origin, owner, u):
        group, split = part(origin, owner)
        return w.at[group, pl.ds(u * size, size), split]

    def ring_copy(way, hop, u):
        origin = lax.rem(spot + hop if way else spot - hop + chips, chips)
        ref = piece(origin, core, u)
        peer = near[1] if way else near[0]
        return remote(ref, ref, ring_sent.at[way, hop - 1, u], ring_got.at[way, hop - 1, u], peer)

    def forward(way, hop, u):
        origin = lax.rem(spot + hop - 1 if way else spot - hop + 1 + chips, chips)
        ref = piece(origin, core, u)
        peer = near[1] if way else near[0]
        return remote(ref, ref, ring_sent.at[way, hop - 1, u], ring_got.at[way, hop - 1, u], peer)

    def pass_copy(origin, owner, u):
        ref = piece(origin, owner, u)
        return remote(ref, ref, pass_sent.at[origin, u], pass_got.at[origin, u], partner)

    def carried(way, hop, u):
        mine = (u < subs // 2) if way == 0 else (u >= subs // 2)
        return (hop < hops) | ((hop == hops) & mine)

    @pl.loop(0, subs)
    def _(u):
        for i in range(size):
            b = u * size + i
            slot = place[b]
            w[my_group, b, my_split] = got[slot // slots, lax.rem(slot, slots)]
        for way in range(2):
            @pl.when(carried(way, 1, u))
            def _():
                forward(way, 1, u).start()
        pass_copy(spot, core, u).start()

    def receive(hop, u):
        for way in range(2):
            @pl.when(carried(way, hop, u))
            def _():
                ring_copy(way, hop, u).wait_recv()
                origin = lax.rem(spot + hop if way else spot - hop + chips, chips)
                pass_copy(origin, core, u).start()

                @pl.when((hop < hops) & carried(way, hop + 1, u))
                def _():
                    forward(way, hop + 1, u).start()

    def shared(origin):
        @pl.loop(0, subs)
        def _(u):
            pass_copy(origin, 1 - core, u).wait_recv()

    def save_copy(group):
        return pltpu.make_async_copy(w.at[group], w_hbm.at[group], save_sem.at[group])

    def begin(head):
        for g in range(2):
            save_copy(2 * head + g).start()
        total[...] = jnp.zeros_like(total)
        step = group_of(blocks)

        @pl.loop(0, blocks // step)
        def _(i):
            ws = [
                w[2 * head + g, pl.ds(i * step, step)].reshape(step * splits * rows, lane)
                for g in range(2)
            ]
            cols = pl.ds(pl.multiple_of(i * step * BR, step * BR), step * BR)
            total[...] += jnp.dot(
                tok[:, cols], jnp.concatenate(ws, axis=1), preferred_element_type=jnp.float32
            )

        key = total[:, :hd]
        rot = key * cos_ref[...] + pltpu.roll(key, hd // 2, 1) * sin_ref[...]
        rot = rot.astype(jnp.bfloat16)
        kv[:, :hd] = rot
        kv[:, hd:] = total[:, hd:].astype(jnp.bfloat16)
        key_t[...] = rot.astype(jnp.float32).T.astype(jnp.bfloat16)
        rot_acc[...] = jnp.zeros_like(rot_acc)
        val_acc[...] = jnp.zeros_like(val_acc)

    def unit(head, j):
        lanes = pl.ds(pl.multiple_of((head * per_head + j) * hd, hd), hd)
        for t in range(tok_count // tile):
            span = slice(t * tile, (t + 1) * tile)
            reach = (t + 1) * tile
            q = q_ref[span, lanes]
            og = og_ref[span, lanes]
            nt = (((1,), (1,)), ((), ()))
            s = lax.dot_general(kv[:reach, :hd], q, nt, preferred_element_type=jnp.float32)
            s = s * (inv_root * LOG2E) + bias[:reach, span]
            e = jnp.exp2(s - jnp.max(s, axis=0, keepdims=True))
            p = e * (1.0 / jnp.sum(e, axis=0, keepdims=True))
            pb = p.astype(jnp.bfloat16)
            dp = lax.dot_general(kv[:reach, hd:], og, nt, preferred_element_type=jnp.float32)
            dot = jnp.sum(pb.astype(jnp.float32) * dp, axis=0, keepdims=True)
            ds = (p * (dp - dot)).astype(jnp.bfloat16)
            val_acc[:reach, :] += jnp.dot(pb, og, preferred_element_type=jnp.float32)
            rot_acc[:reach, :] += jnp.dot(ds, q, preferred_element_type=jnp.float32)
            dq = jnp.dot(key_t[:, :reach], ds, preferred_element_type=jnp.float32)
            dq_ref[span, lanes] = (dq * inv_root).T.astype(jnp.bfloat16)

    def finish(head):
        g = rot_acc[...] * inv_root
        back = g * cos_ref[...] - pltpu.roll(g, hd // 2, 1) * sin_ref[...]
        at = pl.multiple_of(head * 2 * hd, 2 * hd)
        pair_ref[:, pl.ds(at, hd)] = back.astype(jnp.bfloat16)
        pair_ref[:, pl.ds(at + hd, hd)] = val_acc[...].astype(jnp.bfloat16)

    if groups == chips and heads == hops and per_head % subs == 0:
        def head_at(k):
            side = jnp.where(lax.rem(k + spot, 2) == 0, 1, -1)
            return lax.rem(spot // 2 + side * ((k + 1) // 2) + 2 * heads, heads)

        @pl.loop(0, hops + 1)
        def _(t):
            head = head_at(jnp.maximum(t - 1, 0))

            @pl.when(t >= 1)
            def _():
                shared(2 * head)
                shared(2 * head + 1)
                begin(head)

            @pl.loop(0, subs)
            def _(u):
                @pl.when(t < hops)
                def _():
                    receive(t + 1, u)

                @pl.when(t >= 1)
                def _():
                    for i in range(per_head // subs):
                        unit(head, u * (per_head // subs) + i)

            @pl.when(t >= 1)
            def _():
                finish(head)
    else:
        @pl.loop(0, hops)
        def _(t):
            @pl.loop(0, subs)
            def _(u):
                receive(t + 1, u)

        @pl.loop(0, chips)
        def _(origin):
            shared(origin)

        @pl.loop(0, heads)
        def _(head):
            begin(head)

            @pl.loop(0, per_head)
            def _(j):
                unit(head, j)

            finish(head)

    @pl.loop(1, dp_count)
    def _(k):
        swap_copy(k).wait_send()

    @pl.loop(0, subs)
    def _(u):
        @pl.loop(0, chips)
        def _(origin):
            pass_copy(origin, core, u).wait_send()

        @pl.loop(1, hops + 1)
        def _(hop):
            for way in range(2):
                @pl.when(carried(way, hop, u))
                def _():
                    forward(way, hop, u).wait_send()

    @pl.loop(0, groups)
    def _(group):
        save_copy(group).wait()

    save_tok.wait()


def gather_attend(place, slots, tokens, queries, out_grad, seg_row, cos_tab, sin_tab, head_count, dp_count):
    slot_count, _, width = slots.shape
    tok_count, q_width = queries.shape
    chips = dp_count // 2
    lane = width // head_count // 2
    groups = 2 * head_count
    blocks = place.shape[0]
    splits = dp_count // groups
    rows = BR // splits
    subs = 8
    hops = chips // 2
    tile = tok_count // 2 if tok_count % 512 == 0 else tok_count
    bf = jnp.bfloat16
    f32 = jnp.float32
    whole = pl.BlockSpec(memory_space=pltpu.VMEM)
    far = pl.BlockSpec(memory_space=pl.ANY)
    dma = pltpu.SemaphoreType.DMA
    return pl.pallas_call(
        functools.partial(gather_kernel, chips, head_count, subs, tile),
        out_shape=(
            jax.ShapeDtypeStruct((tok_count, q_width), bf),
            jax.ShapeDtypeStruct((tok_count, width), bf),
            jax.ShapeDtypeStruct((groups, blocks, splits, rows, lane), bf),
            jax.ShapeDtypeStruct((blocks, splits, rows, tok_count), bf),
        ),
        in_specs=[pl.BlockSpec(memory_space=pltpu.SMEM), whole, far, far, far] + [whole] * 4,
        out_specs=(whole, whole, far, far),
        scratch_shapes=[
            pltpu.VMEM(tokens.shape, bf),
            pltpu.VMEM(queries.shape, bf),
            pltpu.VMEM(queries.shape, bf),
            pltpu.VMEM((blocks, splits, rows, tok_count), bf),
            pltpu.VMEM((groups, blocks, splits, rows, lane), bf),
            pltpu.VMEM((dp_count, slot_count, rows, lane), bf),
            pltpu.VMEM((tok_count, 2 * lane), f32),
            pltpu.VMEM((tok_count, 2 * lane), bf),
            pltpu.VMEM((tok_count, tok_count), f32),
            pltpu.VMEM((lane, tok_count), bf),
            pltpu.VMEM((tok_count, lane), f32),
            pltpu.VMEM((tok_count, lane), f32),
            dma((3,)),
            dma((groups + 1,)),
            dma((dp_count,)),
            dma((dp_count,)),
            dma((2, hops, subs)),
            dma((2, hops, subs)),
            dma((chips, subs)),
            dma((chips, subs)),
        ],
        compiler_params=pltpu.CompilerParams(
            collective_id=1, has_side_effects=True, vmem_limit_bytes=VMEM_LIMIT
        ),
        cost_estimate=pl.CostEstimate(
            flops=10 * tok_count * tok_count * q_width, bytes_accessed=10**8,
            transcendentals=tok_count * tok_count * q_width // lane,
        ),
        name="gather_attend",
    )(place, slots, tokens, queries, out_grad, seg_row.reshape(-1, 1), seg_row, cos_tab, sin_tab)


def scatter_kernel(
    chips, subs, block_of, used, tok_ref, pair_ref, out_ref,
    part_out, part_in, ring_out, ring_in, final, swap_out, swap_in,
    part_sent, part_got, ring_sent, ring_got, swap_sent, swap_got,
):
    dp_count = 2 * chips
    me = lax.axis_index("dp")
    core = lax.rem(me, 2)
    spot = position_of(chips, me // 2)
    ahead = 2 * chip_at(chips, lax.rem(spot + 1, chips)) + core
    behind = 2 * chip_at(chips, lax.rem(spot + chips - 1, chips)) + core
    partner = me + 1 - 2 * core
    blocks, splits, rows, tok_count = tok_ref.shape
    lane = final.shape[2]
    groups = pair_ref.shape[1] // lane
    per = chips // groups
    half = blocks // 2
    size = half // subs
    slots = swap_out.shape[1]

    meet(dp_count, me)

    def goal(way, step):
        return lax.rem(spot + (chips - 1 - step if way == 0 else 1 + step), chips)

    def product(way, step, owner, u):
        position = goal(way, step)
        split = lax.rem(position, per) * 2 + owner
        left = tok_ref[way * half + u * size : way * half + (u + 1) * size, split]
        lanes = pl.ds(pl.multiple_of((position // per) * lane, lane), lane)
        return jnp.dot(
            left.reshape(size * rows, tok_count), pair_ref[:, lanes],
            preferred_element_type=jnp.float32,
        ).reshape(size, rows, lane)

    def part_copy(way, step):
        return remote(
            part_out.at[way, step], part_in.at[way, step],
            part_sent.at[way, step], part_got.at[way, step], partner,
        )

    def ring_copy(way, step, u):
        at = pl.ds(u * size, size)
        return remote(
            ring_out.at[way, step, at], ring_in.at[way, step, at],
            ring_sent.at[way, step, u], ring_got.at[way, step, u],
            ahead if way == 0 else behind,
        )

    def send_part(step):
        for way in range(2):
            for u in range(subs):
                at = slice(u * size, (u + 1) * size)
                part_out[way, step, at] = product(way, step, 1 - core, u).astype(jnp.bfloat16)
            part_copy(way, step).start()

    def ring_step(step, first, last):
        for way in range(2):
            part_copy(way, step).wait_recv()
        for u in range(subs):
            at = slice(u * size, (u + 1) * size)
            for way in range(2):
                total = product(way, step, core, u) + part_in[way, step, at].astype(jnp.float32)
                if not first:
                    ring_copy(way, step - 1, u).wait_recv()
                    total = total + ring_in[way, step - 1, at].astype(jnp.float32)
                if last:
                    final[way * half + u * size : way * half + (u + 1) * size] = total.astype(
                        jnp.bfloat16
                    )
                else:
                    ring_out[way, step, at] = total.astype(jnp.bfloat16)
                    ring_copy(way, step, u).start()

    send_part(0)
    send_part(1)
    ring_step(0, True, False)

    @pl.loop(1, chips - 1)
    def _(step):
        send_part(step + 1)
        ring_step(step, False, False)

    ring_step(chips - 1, False, True)

    def swap_copy(k):
        peer = lax.rem(me + k, dp_count)
        return remote(swap_out.at[peer], swap_in.at[me], swap_sent.at[k], swap_got.at[k], peer)

    def fill(peer):
        for i in range(slots):
            slot = peer * slots + i
            taken = final[block_of[slot]]
            swap_out[peer, i] = jnp.where(used[slot] != 0, taken, jnp.zeros_like(taken))

    def place_in(origin, value):
        position = position_of(chips, origin // 2)
        split = lax.rem(position, per) * 2 + lax.rem(origin, 2)
        at = pl.ds(pl.multiple_of(split * rows, rows), rows)
        lanes = pl.ds(pl.multiple_of((position // per) * lane, lane), lane)
        out_ref[:, at, lanes] = value.astype(jnp.float32)

    @pl.loop(1, dp_count)
    def _(k):
        fill(lax.rem(me + k, dp_count))
        swap_copy(k).start()

    fill(me)
    place_in(me, swap_out[me])

    @pl.loop(1, dp_count)
    def _(k):
        swap_copy(k).wait_recv()
        origin = lax.rem(me + dp_count - k, dp_count)
        place_in(origin, swap_in[origin])

    @pl.loop(1, dp_count)
    def _(k):
        swap_copy(k).wait_send()

    @pl.loop(0, chips)
    def _(step):
        for way in range(2):
            part_copy(way, step).wait_send()

    @pl.loop(0, chips - 1)
    def _(step):
        for way in range(2):
            for u in range(subs):
                ring_copy(way, step, u).wait_send()


def scatter_sum(tok_pieces, pairs, block_of, used, dp_count):
    chips = dp_count // 2
    width = pairs.shape[1]
    blocks, splits, rows, tok_count = tok_pieces.shape
    lane = width * splits // dp_count
    slots = block_of.shape[0] // dp_count
    subs = 4
    whole = pl.BlockSpec(memory_space=pltpu.VMEM)
    scalars = pl.BlockSpec(memory_space=pltpu.SMEM)
    half = blocks // 2
    bf = jnp.bfloat16
    dma = pltpu.SemaphoreType.DMA
    return pl.pallas_call(
        functools.partial(scatter_kernel, chips, subs),
        out_shape=jax.ShapeDtypeStruct((slots, BR, width), jnp.float32),
        in_specs=[scalars, scalars, whole, whole],
        out_specs=whole,
        scratch_shapes=[
            pltpu.VMEM((2, chips, half, rows, lane), bf),
            pltpu.VMEM((2, chips, half, rows, lane), bf),
            pltpu.VMEM((2, chips - 1, half, rows, lane), bf),
            pltpu.VMEM((2, chips - 1, half, rows, lane), bf),
            pltpu.VMEM((blocks, rows, lane), bf),
            pltpu.VMEM((dp_count, slots, rows, lane), bf),
            pltpu.VMEM((dp_count, slots, rows, lane), bf),
            dma((2, chips)),
            dma((2, chips)),
            dma((2, chips - 1, subs)),
            dma((2, chips - 1, subs)),
            dma((dp_count,)),
            dma((dp_count,)),
        ],
        compiler_params=pltpu.CompilerParams(
            collective_id=0, has_side_effects=True, vmem_limit_bytes=VMEM_LIMIT
        ),
        cost_estimate=pl.CostEstimate(
            flops=16 * tok_pieces.size * width, bytes_accessed=10**8, transcendentals=0
        ),
        name="scatter_sum",
    )(block_of, used, tok_pieces, pairs)


def input_kernel(add, owner, pair_ref, w_ref, *refs):
    out_ref = refs[-1]
    w = jnp.concatenate([w_ref[g] for g in range(w_ref.shape[0])], axis=1)
    total = lax.dot_general(
        pair_ref[...], w, (((1,), (1,)), ((), ())), preferred_element_type=jnp.float32
    )
    if add:
        total = total + refs[0][...].astype(jnp.float32)
    out_ref[...] = total.astype(jnp.bfloat16)


def input_part(pairs, gathered, owner, count, other=None):
    tok_count, width = pairs.shape
    groups, _, lane = gathered.shape
    deep = group_of(count) * BR
    steps = count * BR // deep
    wide = pl.BlockSpec((tok_count, deep), lambda i, p: (0, i))
    add = other is not None
    return pl.pallas_call(
        functools.partial(input_kernel, add),
        out_shape=jax.ShapeDtypeStruct((tok_count, count * BR), jnp.bfloat16),
        grid_spec=pltpu.PrefetchScalarGridSpec(
            num_scalar_prefetch=1,
            grid=(steps,),
            in_specs=[
                pl.BlockSpec(pairs.shape, lambda i, p: (0, 0)),
                pl.BlockSpec((groups, deep, lane), lambda i, p: (0, p[0] * steps + i, 0)),
            ]
            + ([wide] if add else []),
            out_specs=wide,
        ),
        compiler_params=params(),
        cost_estimate=pl.CostEstimate(
            flops=2 * tok_count * width * count * BR,
            bytes_accessed=2 * (count * BR * width + 2 * tok_count * count * BR),
            transcendentals=0,
        ),
        name="input_own" if add else "input_other",
    )(owner.reshape(1), pairs, gathered, *((other,) if add else ()))


def local(tokens, queries, out_grad, segment_ids, weight_slots, old_place, new_place):
    tok_count = tokens.shape[0]
    slot_rows, head_count, _, head_size = weight_slots.shape
    width = head_count * 2 * head_size
    dp_count = lax.axis_size("dp")
    mp_count = lax.axis_size("mp")
    slot_total = dp_count * (slot_rows // BR)
    block_count = old_place.shape[0]

    half = head_size // 2
    frequency = 500000.0 ** (-2.0 * jnp.arange(half, dtype=jnp.float32) / head_size)
    angle = jnp.arange(tok_count, dtype=jnp.float32)[:, None] * frequency[None, :]
    cos_half, sin_half = jnp.cos(angle), jnp.sin(angle)
    cos_tab = jnp.concatenate([cos_half, cos_half], axis=1)
    sin_tab = jnp.concatenate([-sin_half, sin_half], axis=1)

    query_grad, pair_grad, gathered, tok_pieces = gather_attend(
        old_place, weight_slots.reshape(slot_rows // BR, BR, width), tokens,
        queries.reshape(tok_count, -1), out_grad.reshape(tok_count, -1), segment_ids,
        cos_tab, sin_tab, head_count, dp_count,
    )
    gathered = gathered.reshape(2 * head_count, block_count * BR, head_size)

    slot_ids = jnp.arange(slot_total, dtype=jnp.int32)
    matched = (new_place[None, :] == slot_ids[:, None]).astype(jnp.int32)
    block_of = jnp.sum(matched * jnp.arange(block_count, dtype=jnp.int32)[None, :], axis=1)
    used = jnp.sum(matched, axis=1)
    me = lax.axis_index("mp")
    share = block_count // mp_count
    total = None
    for gap in range(1, mp_count):
        target = lax.rem(me + gap, mp_count)
        piece = input_part(pair_grad, gathered, target, share)
        ring = [(i, (i + gap) % mp_count) for i in range(mp_count)]
        arrived = lax.ppermute(piece, "mp", ring)
        total = arrived if total is None else total + arrived
    weight_grad = scatter_sum(tok_pieces, pair_grad, block_of, used, dp_count)
    input_grad = input_part(pair_grad, gathered, me, share, total)
    return (
        input_grad,
        query_grad.reshape(queries.shape),
        weight_grad.reshape(slot_rows, head_count, 2, head_size),
    )


def solution(mesh):
    return jax.shard_map(
        local,
        mesh=mesh,
        in_specs=(
            P("dp", None),
            P("dp", "mp", None),
            P("dp", "mp", None),
            P("dp", None),
            P("dp", "mp", None, None),
            P(),
            P(),
        ),
        out_specs=(P("dp", "mp"), P("dp", "mp", None), P("dp", "mp", None, None)),
        check_vma=False,
    )
```

time: 423 us -> 353 us (0.83)
  waiting for transfers between devices: 132 us -> 0.01 us
  Pallas kernels: 221 us -> 318 us
  local copies, waits for them, and re-layouts: 50.9 us -> 30.6 us
  between operations: 14.1 us -> 0.67 us
    all_gather x1 -> x0, waiting for transfers between devices: 132 us -> none  [local(): lax.all_gather(weight_slots.reshape(slot_rows, width), 'dp', axis=0, tile...]
    pallas_call x4 -> x3, Pallas kernels: 80.1 us -> 175 us  [the longest x1 157 us: gather_attend(): pl.pallas_call(functools.partial(gather_kernel, chips, head_count, subs,...]
    unnamed x8 -> x5, local copies, waits for them, and re-layouts: 17.5 us -> 5.5 us
    transpose x1 -> x0, local copies, waits for them, and re-layouts: 7.63 us -> none  [local(): tokens.reshape(tok_count, block_count, dp_count, short)]
  transfers between devices with their start and end apart: 2 -> 1, of which waited for: 1 -> 0; matrix products, arithmetic and copies ran while one was open for 12% -> 4% of each run, Pallas kernels for 33% -> 40%
where the time goes in v2:
time: 353 us
  Pallas kernels  318 us (90%)
  local copies, waits for them, and re-layouts  30.6 us (9%)
    pallas_call x1, Pallas kernels, gather_attend(): pl.pallas_call(functools.partial(gather_kernel, chips, head_count, subs,...  157 us
    pallas_call x1, Pallas kernels, scatter_sum(): pl.pallas_call(functools.partial(scatter_kernel, chips, subs), out_shape=...  143 us
    pallas_call x2, Pallas kernels, input_part(): pl.pallas_call(functools.partial(input_kernel, add), out_shape=jax.ShapeD...  18.4 us
    reshape x1, local copies, waits for them, and re-layouts, local(): out_grad.reshape(tok_count, -1)  13.2 us
  transfers between devices with their start and end apart: 1, of which 0 were waited for; matrix products, arithmetic and copies ran while one was open for 4% of the time, Pallas kernels for 40%

profile of v2, /device:TPU:11, one launch (start us, length us, event | category | flops | bytes accessed | tf_op | source)
XLA Modules:
  0.0 353.1 jit_solution(11704025096595508659)
XLA Ops:
  0.6 0.0 copy-start
  0.7 4.4 %reshape.40.slots_ref = bf16[8,128,1024]{2,1,0:T(8,128)(2,1)} reshape(bf16[1024,4,2,128]{3,2,1,0:T(2,128)(2,1)} %param.11) | data formatting | bytes 4194304 | tf_op jit(solution)/shard_map/reshape | solution.py:607
  5.1 0.0 copy-done
  5.1 0.9 copy.11.col_ref
  6.0 1.0 fusion.2
  7.0 13.2 %copy_bitcast_fusion = (bf16[512,4096]{1,0:T(8,128)(2,1)}, bf16[512,4096]{1,0:T(8,128)(2,1)}) fusion(bf16[64,8,32,128]{3,2,1,0:T(8,128)(2,1)} %bitcast.16, bf16[64,8,32,128]{3,2,1,0:T(8,128)(2,1)} %bitcast.17), kind=kLoop, calls=%fused_computation | loop fusion | bytes 16777216 | tf_op jit(solution)/shard_map/reshape | solution.py:608
  20.2 1.0 pad_maximum_fusion
  21.2 156.8 %gather_attend.1 = (bf16[512,4096]{1,0:T(8,128)(2,1)}, bf16[512,1024]{1,0:T(8,128)(2,1)}, bf16[8,64,2,64,128]{4,3,2,1,0:T(8,128)(2,1)}, bf16[64,2,64,512]{3,2,1,0:T(8,128)(2,1)}) custom-call(s32[64]{0:T(128)} %place.1, bf16[8,128,1024]{2,1,0:T(8,128)(2,1)} %reshape.40.slots_ref, bf16[512,8192]{1,0:T(8,128)(2,1)} %tok_hbm.1, ...), custom_call_target="tpu_custom_call" | custom-call | flops 10737418240 | bytes 100000000 | tf_op jit(solution)/shard_map/gather_attend/pallas_call | solution.py:332
  178.0 8.9 %input_other.1 = bf16[512,4096]{1,0:T(8,128)(2,1)} custom-call(s32[1]{0:T(128)} %bitcast.3.owner, bf16[512,1024]{1,0:T(8,128)(2,1)} %get-tuple-element.7.pair_ref, bf16[8,8192,128]{2,1,0:T(8,128)(2,1)} %bitcast.12), custom_call_target="tpu_custom_call" | custom-call | flops 4294967296 | bytes 16777216 | tf_op jit(solution)/shard_map/input_other/pallas_call | solution.py:567
  186.9 1.2 collective-permute-start
  188.2 0.0 copy-start.1
  188.2 5.5 %copy.14 = bf16[64,8,32,128]{3,2,1,0:T(8,128)(2,1)} copy(bf16[64,8,32,128]{3,1,2,0:T(8,128)(2,1)} %bitcast.15) | data formatting | bytes 8388608
  193.7 0.0 copy-done.1
  193.7 0.6 convert_reduce_fusion
  194.3 142.7 %scatter_sum.1 = f32[8,128,1024]{2,1,0:T(8,128)} custom-call(s32[128]{0:T(128)} %get-tuple-element.12.block_of, s32[128]{0:T(128)} %get-tuple-element.11.used, bf16[64,2,64,512]{3,2,1,0:T(8,128)(2,1)} %get-tuple-element.10.tok_ref, bf16[512,1024]{1,0:T(8,128)(2,1)} %get-tuple-element.7.pair_ref), custom_call_target="tpu_custom_call" | custom-call | flops 68719476736 | bytes 100000000 | tf_op jit(solution)/shard_map/scatter_sum/pallas_call | solution.py:519
  336.9 6.6 %reshape.47 = f32[1024,4,2,128]{3,2,1,0:T(2,128)} reshape(f32[8,128,1024]{2,1,0:T(8,128)} %scatter_sum.1) | data formatting | bytes 8388608 | tf_op jit(solution)/shard_map/reshape | solution.py:631
  343.5 0.0 collective-permute-done.refs_0_
  343.5 9.5 %input_own.1 = bf16[512,4096]{1,0:T(8,128)(2,1)} custom-call(s32[1]{0:T(128)} %bitcast.owner, bf16[512,1024]{1,0:T(8,128)(2,1)} %get-tuple-element.7.pair_ref, bf16[8,8192,128]{2,1,0:T(8,128)(2,1)} %bitcast.13, bf16[512,4096]{1,0:T(8,128)(2,1)} %collective-permute-done.refs_0_), custom_call_target="tpu_custom_call" | custom-call | flops 4294967296 | bytes 16777216 | tf_op jit(solution)/shard_map/input_own/pallas_call | solution.py:567
  (1 shorter events, 0.0 us)
Async XLA Ops:
  0.6 4.5 %copy-start = (s32[1,512]{1,0:T(1,128)S(1)}, s32[1,512]{1,0:T(1,128)}, u32[]{:S(2)}) copy-start(s32[1,512]{1,0:T(1,128)} %row_ref.1) | copy-start | bytes 6148
  186.9 156.6 %collective-permute-start = (bf16[512,4096]{1,0:T(8,128)(2,1)}, bf16[512,4096]{1,0:T(8,128)(2,1)}, u32[]{:S(2)}, u32[]{:S(2)}) collective-permute-start(bf16[512,4096]{1,0:T(8,128)(2,1)} %input_other.1), channel_id=1, source_target_pairs={{0,1},{1,0},{2,3},{3,2},{4,5},{5,4},{6,7},{7,6},{8,9},{9,8},{10,11... | collective-permute-start | bytes 12582920 | tf_op jit(solution)/shard_map/ppermute | solution.py:624
  188.2 5.5 %copy-start.1 = (s32[64]{0:T(128)S(1)}, s32[64]{0:T(128)}, u32[]{:S(2)}) copy-start(s32[64]{0:T(128)} %param.13) | copy-start | bytes 772

commit v3 on v2

v3 whole, which is shorter than its diff:
```python
import functools

import jax
import jax.numpy as jnp
import numpy as np
from jax import lax
from jax.experimental import pallas as pl
from jax.experimental.pallas import tpu as pltpu
from jax.sharding import PartitionSpec as P

BR = 128
LOG2E = 1.4426950408889634
VMEM_LIMIT = 60 * 1024 * 1024
MESH = pl.DeviceIdType.MESH


def group_of(count):
    for size in (8, 4, 2):
        if count % size == 0:
            return size
    return 1


def chip_at(chips, position):
    return jnp.where(position < chips // 2, 2 * position, 2 * (chips - 1 - position) + 1)


def position_of(chips, chip):
    return jnp.where(lax.rem(chip, 2) == 0, chip // 2, chips - 1 - chip // 2)


def meet(*sizes):
    barrier = pltpu.get_barrier_semaphore()
    for axis, count in sizes:
        me = lax.axis_index(axis)

        @pl.loop(1, count)
        def _(k):
            pl.semaphore_signal(
                barrier, inc=1, device_id={axis: lax.rem(me + k, count)}, device_id_type=MESH
            )

    pl.semaphore_wait(barrier, sum(count - 1 for _, count in sizes))


def remote(src, dst, sent, got, peer, axis="dp"):
    return pltpu.make_async_remote_copy(
        src_ref=src, dst_ref=dst, send_sem=sent, recv_sem=got,
        device_id={axis: peer}, device_id_type=MESH,
    )


def gather_kernel(
    chips, heads, subs, tile, place, slots_ref, tok_hbm, q_hbm, og_hbm, row_ref,
    freq_ref, dq_ref, pair_ref, w_hbm, tokt_hbm,
    tok, q_ref, og_ref, stage, tokt, w, got, total, kv, bias, key_t, rot_acc, val_acc,
    cos_ref, sin_ref, load_sem, stage_sem, save_sem, swap_sent, swap_got, ring_sent, ring_got, pass_sent, pass_got,
):
    dp_count = 2 * chips
    hops = chips // 2
    me = lax.axis_index("dp")
    core = lax.rem(me, 2)
    spot = position_of(chips, me // 2)
    partner = me + 1 - 2 * core
    groups, blocks, splits, rows, lane = w.shape
    per = chips // groups
    slots = slots_ref.shape[0]
    tok_count, hd = tok.shape[0], lane
    per_head = q_ref.shape[0] // heads
    near = (
        2 * chip_at(chips, lax.rem(spot + 1, chips)) + core,
        2 * chip_at(chips, lax.rem(spot + chips - 1, chips)) + core,
    )
    size = blocks // subs
    inv_root = 1.0 / (hd ** 0.5)

    load = pltpu.make_async_copy(tok_hbm, tok, load_sem)
    load.start()
    band = stage.shape[1]
    bands = tok_count // band

    def stage_copy(src, i, slot):
        return pltpu.make_async_copy(src.at[pl.ds(i * band, band)], stage.at[slot], stage_sem.at[slot])

    stage_copy(q_hbm, 0, 0).start()
    stage_copy(og_hbm, 0, 1).start()

    def part(position, owner):
        return position // per, lax.rem(position, per) * 2 + owner

    meet(("dp", dp_count))

    def swap_copy(k):
        peer = lax.rem(me + k, dp_count)
        group, split = part(position_of(chips, peer // 2), lax.rem(peer, 2))
        src = slots_ref.at[
            :, pl.ds(pl.multiple_of(split * rows, rows), rows),
            pl.ds(pl.multiple_of(group * lane, lane), lane),
        ]
        return remote(src, got.at[me], swap_sent.at[k], swap_got.at[k], peer)

    @pl.loop(1, dp_count)
    def _(k):
        swap_copy(k).start()

    my_group, my_split = part(spot, core)
    own_rows = pl.ds(pl.multiple_of(my_split * rows, rows), rows)
    own_lanes = pl.ds(pl.multiple_of(my_group * lane, lane), lane)
    got[me] = slots_ref[:, own_rows, own_lanes]

    kpos = lax.broadcasted_iota(jnp.int32, bias.shape, 0)
    qpos = lax.broadcasted_iota(jnp.int32, bias.shape, 1)
    ids = jnp.broadcast_to(row_ref[...].astype(jnp.float32), bias.shape)
    bias[...] = ids.T
    allowed = (kpos <= qpos) & (bias[...] == ids)
    bias[...] = jnp.where(allowed, 0.0, -1e30).astype(jnp.float32)
    spots = lax.broadcasted_iota(jnp.int32, cos_ref.shape, 0).astype(jnp.float32)
    lower = lax.broadcasted_iota(jnp.int32, cos_ref.shape, 1) < hd // 2
    angle = spots * freq_ref[...]
    cos_ref[...] = jnp.cos(angle)
    sine = jnp.sin(angle)
    sin_ref[...] = jnp.where(lower, -sine, sine)

    @pl.loop(0, bands)
    def _(i):
        at = pl.ds(pl.multiple_of(i * band, band), band)
        for slot, (src, dst) in enumerate(((q_hbm, q_ref), (og_hbm, og_ref))):
            stage_copy(src, i, slot).wait()
            dst[:, at, :] = pltpu.einshape("thd->htd", stage[slot])

            @pl.when(i + 1 < bands)
            def _():
                stage_copy(src, i + 1, slot).start()

    load.wait()

    @pl.loop(0, blocks)
    def _(b):
        cols = tok[:, pl.ds(pl.multiple_of(b * BR, BR), BR)]
        flipped = cols.astype(jnp.float32).T
        tokt[b] = flipped.reshape(splits, rows, tok_count).astype(jnp.bfloat16)

    save_tok = pltpu.make_async_copy(tokt, tokt_hbm, save_sem.at[groups])
    save_tok.start()

    @pl.loop(1, dp_count)
    def _(k):
        swap_copy(k).wait_recv()

    def piece(origin, owner, u):
        group, split = part(origin, owner)
        return w.at[group, pl.ds(u * size, size), split]

    def ring_copy(way, hop, u):
        origin = lax.rem(spot + hop if way else spot - hop + chips, chips)
        ref = piece(origin, core, u)
        peer = near[1] if way else near[0]
        return remote(ref, ref, ring_sent.at[way, hop - 1, u], ring_got.at[way, hop - 1, u], peer)

    def forward(way, hop, u):
        origin = lax.rem(spot + hop - 1 if way else spot - hop + 1 + chips, chips)
        ref = piece(origin, core, u)
        peer = near[1] if way else near[0]
        return remote(ref, ref, ring_sent.at[way, hop - 1, u], ring_got.at[way, hop - 1, u], peer)

    def pass_copy(origin, owner, u):
        ref = piece(origin, owner, u)
        return remote(ref, ref, pass_sent.at[origin, u], pass_got.at[origin, u], partner)

    def carried(way, hop, u):
        mine = (u < subs // 2) if way == 0 else (u >= subs // 2)
        return (hop < hops) | ((hop == hops) & mine)

    @pl.loop(0, subs)
    def _(u):
        for i in range(size):
            b = u * size + i
            slot = place[b]
            w[my_group, b, my_split] = got[slot // slots, lax.rem(slot, slots)]
        for way in range(2):
            @pl.when(carried(way, 1, u))
            def _():
                forward(way, 1, u).start()
        pass_copy(spot, core, u).start()

    def receive(hop, u):
        for way in range(2):
            @pl.when(carried(way, hop, u))
            def _():
                ring_copy(way, hop, u).wait_recv()
                origin = lax.rem(spot + hop if way else spot - hop + chips, chips)
                pass_copy(origin, core, u).start()

                @pl.when((hop < hops) & carried(way, hop + 1, u))
                def _():
                    forward(way, hop + 1, u).start()

    def shared(origin):
        @pl.loop(0, subs)
        def _(u):
            pass_copy(origin, 1 - core, u).wait_recv()

    def save_copy(group):
        return pltpu.make_async_copy(w.at[group], w_hbm.at[group], save_sem.at[group])

    def begin(head):
        for g in range(2):
            save_copy(2 * head + g).start()
        total[...] = jnp.zeros_like(total)
        step = group_of(blocks)

        @pl.loop(0, blocks // step)
        def _(i):
            ws = [
                w[2 * head + g, pl.ds(i * step, step)].reshape(step * splits * rows, lane)
                for g in range(2)
            ]
            cols = pl.ds(pl.multiple_of(i * step * BR, step * BR), step * BR)
            total[...] += jnp.dot(
                tok[:, cols], jnp.concatenate(ws, axis=1), preferred_element_type=jnp.float32
            )

        key = total[:, :hd]
        rot = key * cos_ref[...] + pltpu.roll(key, hd // 2, 1) * sin_ref[...]
        rot = rot.astype(jnp.bfloat16)
        kv[:, :hd] = rot
        kv[:, hd:] = total[:, hd:].astype(jnp.bfloat16)
        key_t[...] = rot.astype(jnp.float32).T.astype(jnp.bfloat16)
        rot_acc[...] = jnp.zeros_like(rot_acc)
        val_acc[...] = jnp.zeros_like(val_acc)

    def unit(head, t):
        span = slice(t * tile, (t + 1) * tile)
        lo, reach = max(0, t * tile - tok_count // 2), (t + 1) * tile
        stack = pl.ds(head * per_head, per_head)
        q = q_ref[stack, span, :].reshape(per_head * tile, hd)
        og = og_ref[stack, span, :].reshape(per_head * tile, hd)
        nt = (((1,), (1,)), ((), ()))
        s = lax.dot_general(kv[lo:reach, :hd], q, nt, preferred_element_type=jnp.float32)
        s = s * (inv_root * LOG2E) + jnp.concatenate([bias[lo:reach, span]] * per_head, axis=1)
        e = jnp.exp2(s - jnp.max(s, axis=0, keepdims=True))
        p = e * (1.0 / jnp.sum(e, axis=0, keepdims=True))
        pb = p.astype(jnp.bfloat16)
        dp = lax.dot_general(kv[lo:reach, hd:], og, nt, preferred_element_type=jnp.float32)
        dot = jnp.sum(pb.astype(jnp.float32) * dp, axis=0, keepdims=True)
        ds = (p * (dp - dot)).astype(jnp.bfloat16)
        val_acc[lo:reach, :] += jnp.dot(pb, og, preferred_element_type=jnp.float32)
        rot_acc[lo:reach, :] += jnp.dot(ds, q, preferred_element_type=jnp.float32)
        dq = jnp.dot(key_t[:, lo:reach], ds, preferred_element_type=jnp.float32)
        dq = (dq * inv_root).T.astype(jnp.bfloat16).reshape(per_head, tile, hd)
        dq_ref[span, pl.ds(pl.multiple_of(head * per_head, per_head), per_head), :] = (
            pltpu.einshape("htd->thd", dq)
        )

    def finish(head):
        g = rot_acc[...] * inv_root
        back = g * cos_ref[...] - pltpu.roll(g, hd // 2, 1) * sin_ref[...]
        at = pl.multiple_of(head * 2 * hd, 2 * hd)
        pair_ref[:, pl.ds(at, hd)] = back.astype(jnp.bfloat16)
        pair_ref[:, pl.ds(at + hd, hd)] = val_acc[...].astype(jnp.bfloat16)

    tiles = tok_count // tile
    if groups == chips and heads == hops and subs % tiles == 0:
        def head_at(k):
            side = jnp.where(lax.rem(k + spot, 2) == 0, 1, -1)
            return lax.rem(spot // 2 + side * ((k + 1) // 2) + 2 * heads, heads)

        @pl.loop(0, hops + 1)
        def _(t):
            head = head_at(jnp.maximum(t - 1, 0))

            @pl.when(t >= 1)
            def _():
                shared(2 * head)
                shared(2 * head + 1)
                begin(head)

            for i in range(tiles):
                @pl.when(t < hops)
                def _():
                    @pl.loop(i * (subs // tiles), (i + 1) * (subs // tiles))
                    def _(u):
                        receive(t + 1, u)

                @pl.when(t >= 1)
                def _():
                    unit(head, i)

            @pl.when(t >= 1)
            def _():
                finish(head)
    else:
        @pl.loop(0, hops)
        def _(t):
            @pl.loop(0, subs)
            def _(u):
                receive(t + 1, u)

        @pl.loop(0, chips)
        def _(origin):
            shared(origin)

        @pl.loop(0, heads)
        def _(head):
            begin(head)

            for i in range(tiles):
                unit(head, i)

            finish(head)

    @pl.loop(1, dp_count)
    def _(k):
        swap_copy(k).wait_send()

    @pl.loop(0, subs)
    def _(u):
        @pl.loop(0, chips)
        def _(origin):
            pass_copy(origin, core, u).wait_send()

        @pl.loop(1, hops + 1)
        def _(hop):
            for way in range(2):
                @pl.when(carried(way, hop, u))
                def _():
                    forward(way, hop, u).wait_send()

    @pl.loop(0, groups)
    def _(group):
        save_copy(group).wait()

    save_tok.wait()


def gather_attend(place, slots, tokens, queries, out_grad, seg_row, head_count, dp_count):
    slot_count, _, width = slots.shape
    tok_count = queries.shape[0]
    q_width = queries.shape[1] * queries.shape[2]
    chips = dp_count // 2
    lane = width // head_count // 2
    groups = 2 * head_count
    blocks = place.shape[0]
    splits = dp_count // groups
    rows = BR // splits
    subs = 8
    hops = chips // 2
    tile = 128
    powers = np.power(500000.0, -2.0 * np.arange(lane // 2) / lane)
    frequency = np.concatenate([powers, powers]).astype(np.float32)[None, :]
    turned = (queries.shape[1], tok_count, lane)
    bf = jnp.bfloat16
    f32 = jnp.float32
    whole = pl.BlockSpec(memory_space=pltpu.VMEM)
    far = pl.BlockSpec(memory_space=pl.ANY)
    dma = pltpu.SemaphoreType.DMA
    return pl.pallas_call(
        functools.partial(gather_kernel, chips, head_count, subs, tile),
        out_shape=(
            jax.ShapeDtypeStruct(queries.shape, bf),
            jax.ShapeDtypeStruct((tok_count, width), bf),
            jax.ShapeDtypeStruct((groups, blocks, splits, rows, lane), bf),
            jax.ShapeDtypeStruct((blocks, splits, rows, tok_count), bf),
        ),
        in_specs=[pl.BlockSpec(memory_space=pltpu.SMEM), whole, far, far, far, whole, whole],
        out_specs=(whole, whole, far, far),
        scratch_shapes=[
            pltpu.VMEM(tokens.shape, bf),
            pltpu.VMEM(turned, bf),
            pltpu.VMEM(turned, bf),
            pltpu.VMEM((2, tile) + queries.shape[1:], bf),
            pltpu.VMEM((blocks, splits, rows, tok_count), bf),
            pltpu.VMEM((groups, blocks, splits, rows, lane), bf),
            pltpu.VMEM((dp_count, slot_count, rows, lane), bf),
            pltpu.VMEM((tok_count, 2 * lane), f32),
            pltpu.VMEM((tok_count, 2 * lane), bf),
            pltpu.VMEM((tok_count, tok_count), f32),
            pltpu.VMEM((lane, tok_count), bf),
            pltpu.VMEM((tok_count, lane), f32),
            pltpu.VMEM((tok_count, lane), f32),
            pltpu.VMEM((tok_count, lane), f32),
            pltpu.VMEM((tok_count, lane), f32),
            dma,
            dma((2,)),
            dma((groups + 1,)),
            dma((dp_count,)),
            dma((dp_count,)),
            dma((2, hops, subs)),
            dma((2, hops, subs)),
            dma((chips, subs)),
            dma((chips, subs)),
        ],
        compiler_params=pltpu.CompilerParams(
            collective_id=1, has_side_effects=True, vmem_limit_bytes=VMEM_LIMIT
        ),
        cost_estimate=pl.CostEstimate(
            flops=10 * tok_count * tok_count * q_width, bytes_accessed=10**8,
            transcendentals=tok_count * tok_count * q_width // lane,
        ),
        name="gather_attend",
    )(place, slots, tokens, queries, out_grad, seg_row, frequency)


def scatter_kernel(
    chips, mp_count, subs, block_of, used, tok_hbm, pair_ref, w_hbm, out_ref, in_ref, tok_ref,
    part_out, part_in, ring_out, ring_in, ready, final, swap_out, swap_in, wbuf, side_out, side_in,
    part_sent, part_got, ring_sent, ring_got, swap_sent, swap_got, tok_sem, load_sem, side_sent, side_got,
):
    dp_count = 2 * chips
    me, my = lax.axis_index("dp"), lax.axis_index("mp")
    core = lax.rem(me, 2)
    spot = position_of(chips, me // 2)
    ahead = 2 * chip_at(chips, lax.rem(spot + 1, chips)) + core
    behind = 2 * chip_at(chips, lax.rem(spot + chips - 1, chips)) + core
    partner = me + 1 - 2 * core
    blocks, splits, rows, tok_count = tok_ref.shape
    lane = final.shape[2]
    groups = pair_ref.shape[1] // lane
    per = chips // groups
    half = blocks // 2
    size = half // subs
    slots = swap_out.shape[1]
    keep, early = part_out.shape[1], part_out.shape[1] - 1
    deep = wbuf.shape[2]
    features = in_ref.shape[1]
    chunks = features // deep
    others, units = (mp_count - 1) * chunks, mp_count * chunks

    def load_copy(k):
        target = lax.rem(my + 1 + k // chunks, mp_count)
        start = pl.multiple_of(target * features + lax.rem(k, chunks) * deep, deep)
        slot = lax.rem(k, 2)
        return pltpu.make_async_copy(
            w_hbm.at[:, pl.ds(start, deep), :], wbuf.at[slot], load_sem.at[slot]
        )

    loads = [
        pltpu.make_async_copy(
            tok_hbm.at[pl.ds(i * half, half)], tok_ref.at[pl.ds(i * half, half)], tok_sem.at[i]
        )
        for i in range(2)
    ]
    for load in loads:
        load.start()
    load_copy(0).start()
    meet(("dp", dp_count), ("mp", mp_count))

    def goal(way, step):
        return lax.rem(spot + (chips - 1 - step if way == 0 else 1 + step), chips)

    def product(way, step, owner, u):
        position = goal(way, step)
        split = lax.rem(position, per) * 2 + owner
        left = tok_ref[way * half + u * size : way * half + (u + 1) * size, split]
        lanes = pl.ds(pl.multiple_of((position // per) * lane, lane), lane)
        return jnp.dot(
            left.reshape(size * rows, tok_count), pair_ref[:, lanes],
            preferred_element_type=jnp.float32,
        ).reshape(size, rows, lane)

    def part_copy(way, step):
        return remote(
            part_out.at[way, lax.rem(step, keep)], part_in.at[way, step],
            part_sent.at[way, step], part_got.at[way, step], partner,
        )

    def ring_copy(way, step, u):
        at = pl.ds(u * size, size)
        return remote(
            ring_out.at[way, lax.rem(step, 2), at], ring_in.at[way, step, at],
            ring_sent.at[way, step, u], ring_got.at[way, step, u],
            ahead if way == 0 else behind,
        )

    def span(u):
        return slice(u * size, (u + 1) * size)

    def part_fill(step, way, u):
        part_out[way, lax.rem(step, keep), span(u)] = product(way, step, 1 - core, u).astype(
            jnp.bfloat16
        )

    def ready_fill(step, way, u):
        ready[way, span(u)] = product(way, step, core, u) + part_in[way, step, span(u)].astype(
            jnp.float32
        )

    def ring_step(step, last):
        if not last:
            for way in range(2):
                part_copy(way, step + 1).wait_recv()

            @pl.when(step + early < chips)
            def _():
                for way in range(2):
                    part_copy(way, step - 1).wait_send()

        for u in range(subs):
            for way in range(2):
                ring_copy(way, step - 1, u).wait_recv()
                total = ready[way, span(u)] + ring_in[way, step - 1, span(u)].astype(jnp.float32)
                if last:
                    final[way * half + u * size : way * half + (u + 1) * size] = total.astype(
                        jnp.bfloat16
                    )
                else:
                    @pl.when(step >= 2)
                    def _():
                        ring_copy(way, step - 2, u).wait_send()

                    ring_out[way, lax.rem(step, 2), span(u)] = total.astype(jnp.bfloat16)
                    ring_copy(way, step, u).start()
                    ready_fill(step + 1, way, u)

                    @pl.when(step + early < chips)
                    def _():
                        part_fill(step + early, way, u)
        if not last:
            @pl.when(step + early < chips)
            def _():
                for way in range(2):
                    part_copy(way, step + early).start()

    def side_copy(k):
        target = lax.rem(my + 1 + k // chunks, mp_count)
        return remote(
            side_out.at[k], side_in.at[k], side_sent.at[k], side_got.at[k], target, "mp"
        )

    def unit(k):
        load_copy(k).wait()

        @pl.when(k + 1 < units)
        def _():
            load_copy(k + 1).start()

        slot = lax.rem(k, 2)
        w = jnp.concatenate([wbuf[slot, g] for g in range(groups)], axis=1)
        value = lax.dot_general(
            pair_ref[...], w, (((1,), (1,)), ((), ())), preferred_element_type=jnp.float32
        )

        @pl.when(k < others)
        def _():
            side_out[k] = value.astype(jnp.bfloat16)
            side_copy(k).start()

        @pl.when(k >= others)
        def _():
            chunk = k - others
            total = value
            for gap in range(mp_count - 1):
                side_copy(gap * chunks + chunk).wait_recv()
                total = total + side_in[gap * chunks + chunk].astype(jnp.float32)
            in_ref[:, pl.ds(pl.multiple_of(chunk * deep, deep), deep)] = total.astype(jnp.bfloat16)

    for load in loads:
        load.wait()
    for way in range(2):
        for u in range(subs):
            part_fill(0, way, u)
        part_copy(way, 0).start()
    for way in range(2):
        for u in range(subs):
            ready[way, span(u)] = product(way, 0, core, u)
    for way in range(2):
        part_copy(way, 0).wait_recv()
    for u in range(subs):
        for way in range(2):
            total = ready[way, span(u)] + part_in[way, 0, span(u)].astype(jnp.float32)
            ring_out[way, 0, span(u)] = total.astype(jnp.bfloat16)
            ring_copy(way, 0, u).start()
    for step in range(1, early + 1):
        for way in range(2):
            for u in range(subs):
                part_fill(step, way, u)
            part_copy(way, step).start()
    for way in range(2):
        part_copy(way, 1).wait_recv()
        for u in range(subs):
            ready_fill(1, way, u)
    pace = 2

    @pl.loop(1, chips - 1)
    def _(step):
        ring_step(step, False)

        @pl.loop((step - 1) * pace, step * pace)
        def _(k):
            @pl.when(k < units)
            def _():
                unit(k)

    ring_step(chips - 1, True)

    def swap_copy(k):
        peer = lax.rem(me + k, dp_count)
        return remote(swap_out.at[peer], swap_in.at[me], swap_sent.at[k], swap_got.at[k], peer)

    def fill(peer):
        for i in range(slots):
            slot = peer * slots + i
            taken = final[block_of[slot]]
            swap_out[peer, i] = jnp.where(used[slot] != 0, taken, jnp.zeros_like(taken))

    def place_in(origin, value):
        position = position_of(chips, origin // 2)
        split = lax.rem(position, per) * 2 + lax.rem(origin, 2)
        for i in range(slots):
            start = (i * BR + split * rows) * groups + position // per
            out_ref[pl.ds(start, rows, stride=groups), :] = value[i].astype(jnp.float32)

    @pl.loop(1, dp_count)
    def _(k):
        fill(lax.rem(me + k, dp_count))
        swap_copy(k).start()

    fill(me)
    place_in(me, swap_out[me])

    @pl.loop(min((chips - 2) * pace, units), units)
    def _(k):
        unit(k)

    @pl.loop(1, dp_count)
    def _(k):
        swap_copy(k).wait_recv()
        origin = lax.rem(me + dp_count - k, dp_count)
        place_in(origin, swap_in[origin])

    @pl.loop(1, dp_count)
    def _(k):
        swap_copy(k).wait_send()

    @pl.loop(0, others)
    def _(k):
        side_copy(k).wait_send()

    @pl.loop(max(chips - keep, 0), chips)
    def _(step):
        for way in range(2):
            part_copy(way, step).wait_send()

    @pl.loop(max(chips - 3, 0), chips - 1)
    def _(step):
        for way in range(2):
            for u in range(subs):
                ring_copy(way, step, u).wait_send()


def scatter_sum(tok_pieces, pairs, gathered, block_of, used, dp_count, mp_count):
    chips = dp_count // 2
    width = pairs.shape[1]
    blocks, splits, rows, tok_count = tok_pieces.shape
    groups, lane = gathered.shape[0], gathered.shape[2]
    slots = block_of.shape[0] // dp_count
    subs = 4
    keep = 4
    whole = pl.BlockSpec(memory_space=pltpu.VMEM)
    scalars = pl.BlockSpec(memory_space=pltpu.SMEM)
    far = pl.BlockSpec(memory_space=pl.ANY)
    half = blocks // 2
    features = blocks * BR // mp_count
    deep = group_of(features // BR) // 2 * BR
    others = (mp_count - 1) * features // deep
    bf = jnp.bfloat16
    dma = pltpu.SemaphoreType.DMA
    return pl.pallas_call(
        functools.partial(scatter_kernel, chips, mp_count, subs),
        out_shape=(
            jax.ShapeDtypeStruct((slots * BR * groups, lane), jnp.float32),
            jax.ShapeDtypeStruct((tok_count, features), bf),
        ),
        in_specs=[scalars, scalars, far, whole, far],
        out_specs=(whole, whole),
        scratch_shapes=[
            pltpu.VMEM(tok_pieces.shape, bf),
            pltpu.VMEM((2, keep, half, rows, lane), bf),
            pltpu.VMEM((2, chips, half, rows, lane), bf),
            pltpu.VMEM((2, 2, half, rows, lane), bf),
            pltpu.VMEM((2, chips - 1, half, rows, lane), bf),
            pltpu.VMEM((2, half, rows, lane), jnp.float32),
            pltpu.VMEM((blocks, rows, lane), bf),
            pltpu.VMEM((dp_count, slots, rows, lane), bf),
            pltpu.VMEM((dp_count, slots, rows, lane), bf),
            pltpu.VMEM((2, groups, deep, lane), bf),
            pltpu.VMEM((others, tok_count, deep), bf),
            pltpu.VMEM((others, tok_count, deep), bf),
            dma((2, chips)),
            dma((2, chips)),
            dma((2, chips - 1, subs)),
            dma((2, chips - 1, subs)),
            dma((dp_count,)),
            dma((dp_count,)),
            dma((2,)),
            dma((2,)),
            dma((others,)),
            dma((others,)),
        ],
        compiler_params=pltpu.CompilerParams(
            collective_id=0, has_side_effects=True, vmem_limit_bytes=VMEM_LIMIT
        ),
        cost_estimate=pl.CostEstimate(
            flops=16 * tok_pieces.size * width, bytes_accessed=10**8, transcendentals=0
        ),
        name="scatter_sum",
    )(block_of, used, tok_pieces, pairs, gathered)


def local(tokens, queries, out_grad, segment_ids, weight_slots, old_place, new_place):
    tok_count = tokens.shape[0]
    slot_rows, head_count, _, head_size = weight_slots.shape
    width = head_count * 2 * head_size
    dp_count = lax.axis_size("dp")
    mp_count = lax.axis_size("mp")
    slot_total = dp_count * (slot_rows // BR)
    block_count = old_place.shape[0]

    query_grad, pair_grad, gathered, tok_pieces = gather_attend(
        old_place, weight_slots.reshape(slot_rows // BR, BR, width), tokens,
        queries, out_grad, segment_ids, head_count, dp_count,
    )
    gathered = gathered.reshape(2 * head_count, block_count * BR, head_size)

    slot_ids = jnp.arange(slot_total, dtype=jnp.int32)
    matched = (new_place[None, :] == slot_ids[:, None]).astype(jnp.int32)
    block_of = jnp.sum(matched * jnp.arange(block_count, dtype=jnp.int32)[None, :], axis=1)
    used = jnp.sum(matched, axis=1)
    weight_grad, input_grad = scatter_sum(
        tok_pieces, pair_grad, gathered, block_of, used, dp_count, mp_count
    )
    return (
        input_grad,
        query_grad,
        weight_grad.reshape(slot_rows, head_count, 2, head_size),
    )


def solution(mesh):
    return jax.shard_map(
        local,
        mesh=mesh,
        in_specs=(
            P("dp", None),
            P("dp", "mp", None),
            P("dp", "mp", None),
            P("dp", None),
            P("dp", "mp", None, None),
            P(),
            P(),
        ),
        out_specs=(P("dp", "mp"), P("dp", "mp", None), P("dp", "mp", None, None)),
        check_vma=False,
    )
```

time: 353 us -> 310 us (0.88)
  Pallas kernels: 318 us -> 292 us
  local copies, waits for them, and re-layouts: 30.6 us -> 15 us
    reshape x3 -> x0, local copies, waits for them, and re-layouts: 20.7 us -> none  [the longest x1 13.2 us: local(): out_grad.reshape(tok_count, -1)]
    pallas_call x3 -> x1, Pallas kernels: 161 us -> 143 us  [scatter_sum(): pl.pallas_call(functools.partial(scatter_kernel, chips, mp_count, subs),...]
    pallas_call x1, Pallas kernels: 157 us -> 150 us  [gather_attend(): pl.pallas_call(functools.partial(gather_kernel, chips, head_count, subs,...]
    unnamed x5 -> x7, local copies, waits for them, and re-layouts: 5.5 us -> 10.6 us
  transfers between devices with their start and end apart: 1 -> 0, of which waited for: 0 -> 0; matrix products, arithmetic and copies ran while one was open for 4% -> 0% of each run, Pallas kernels for 40% -> 0%
where the time goes in v3:
time: 310 us; the launch traced here: 309 us
  Pallas kernels  292 us (94%)
  local copies, waits for them, and re-layouts  15 us (5%)
    pallas_call x1, Pallas kernels, gather_attend(): pl.pallas_call(functools.partial(gather_kernel, chips, head_count, subs,...  150 us
    pallas_call x1, Pallas kernels, scatter_sum(): pl.pallas_call(functools.partial(scatter_kernel, chips, mp_count, subs),...  143 us
    unnamed x7, local copies, waits for them, and re-layouts  10.6 us

profile of v3, /device:TPU:11, one launch (start us, length us, event | category | flops | bytes accessed | tf_op | source)
XLA Modules:
  0.0 309.4 jit_solution(4976183998746295949)
XLA Ops:
  0.6 1.3 convert_reduce_fusion
  1.9 4.4 %reshape.16.slots_ref = bf16[8,128,1024]{2,1,0:T(8,128)(2,1)} reshape(bf16[1024,4,2,128]{3,2,1,0:T(2,128)(2,1)} %param.12) | data formatting | bytes 4194304 | tf_op jit(solution)/shard_map/reshape | solution.py:720
  6.3 149.9 %gather_attend.1 = (bf16[512,32,128]{2,1,0:T(8,128)(2,1)}, bf16[512,1024]{1,0:T(8,128)(2,1)}, bf16[8,64,2,64,128]{4,3,2,1,0:T(8,128)(2,1)}, bf16[64,2,64,512]{3,2,1,0:T(8,128)(2,1)}) custom-call(s32[64]{0:T(128)} %place.1, bf16[8,128,1024]{2,1,0:T(8,128)(2,1)} %reshape.16.slots_ref, bf16[512,8192]{1,0:T(8,128)(2,1)} %tok_hbm.1, bf16[512,32,128]{2,1,0:T(8,128)(2,1)} %q_hbm.1, ...), custom_call_target="tpu_custom_call" | custom-call | flops 10737418240 | bytes 100000000 | tf_op jit(solution)/shard_map/gather_attend/pallas_call | solution.py:357
  156.2 142.5 %scatter_sum.1 = (f32[8192,128]{1,0:T(8,128)}, bf16[512,4096]{1,0:T(8,128)(2,1)}) custom-call(s32[128]{0:T(128)} %get-tuple-element.16.block_of, s32[128]{0:T(128)} %get-tuple-element.15.used, bf16[64,2,64,512]{3,2,1,0:T(8,128)(2,1)} %get-tuple-element.9.tok_hbm, bf16[512,1024]{1,0:T(8,128)(2,1)} %get-tuple-element.10.pair_ref, bf16[8,8192,128]{2,1,0:T(8,128)(2,1)} %bitcast.3), custom_call_target="tpu_custom_call" | custom-call | flops 68719476736 | bytes 100000000 | tf_op jit(solution)/shard_map/scatter_sum/pallas_call | solution.py:668
  298.8 0.0 copy-start
  298.8 4.8 %copy.14 = bf16[512,4096]{1,0:T(8,128)(2,1)} copy(bf16[512,4096]{1,0:T(8,128)(2,1)} %get-tuple-element.20) | data formatting | bytes 8388608
  303.6 0.0 copy-done
  303.6 0.0 copy-start.1
  303.7 2.1 copy.15
  305.8 1.6 copy-done.1
  307.4 2.0 copy.16
Async XLA Ops:
  298.8 4.9 %copy-start = (bf16[512,32,128]{2,1,0:T(8,128)(2,1)S(1)}, bf16[512,32,128]{2,1,0:T(8,128)(2,1)}, u32[]{:S(2)}) copy-start(bf16[512,32,128]{2,1,0:T(8,128)(2,1)} %get-tuple-element.21) | copy-start | bytes 12582916
  303.6 3.7 %copy-start.1 = (f32[8192,128]{1,0:T(8,128)S(1)}, f32[8192,128]{1,0:T(8,128)}, u32[]{:S(2)}) copy-start(f32[8192,128]{1,0:T(8,128)} %get-tuple-element.14) | copy-start | bytes 12582916

commit v4 on v3

--- a/solution.py
+++ b/solution.py
@@ -10,7 +10,7 @@
 
 BR = 128
 LOG2E = 1.4426950408889634
-VMEM_LIMIT = 60 * 1024 * 1024
+VMEM_LIMIT = 63 * 1024 * 1024
 MESH = pl.DeviceIdType.MESH
 
 
@@ -51,10 +51,11 @@
 
 
 def gather_kernel(
-    chips, heads, subs, tile, place, slots_ref, tok_hbm, q_hbm, og_hbm, row_ref,
-    freq_ref, dq_ref, pair_ref, w_hbm, tokt_hbm,
+    chips, heads, subs, tile, place, native, tok_hbm, q_hbm, og_hbm, row_ref,
+    freq_ref, dq_ref, pair_ref, w_hbm, tokt_hbm, first_hbm,
     tok, q_ref, og_ref, stage, tokt, w, got, total, kv, bias, key_t, rot_acc, val_acc,
     cos_ref, sin_ref, load_sem, stage_sem, save_sem, swap_sent, swap_got, ring_sent, ring_got, pass_sent, pass_got,
+    near_out, near_in, first_out, first_in, near_sent, near_got, first_sent, first_got, slots_ref,
 ):
     dp_count = 2 * chips
     hops = chips // 2
@@ -84,6 +85,11 @@
 
     stage_copy(q_hbm, 0, 0).start()
     stage_copy(og_hbm, 0, 1).start()
+
+    for i in range(slots):
+        turned = pltpu.einshape("rgd->grd", native[i])
+        for g in range(groups):
+            slots_ref[i, :, g * lane : (g + 1) * lane] = turned[g]
 
     def part(position, owner):
         return position // per, lax.rem(position, per) * 2 + owner
@@ -259,8 +265,45 @@
         pair_ref[:, pl.ds(at, hd)] = back.astype(jnp.bfloat16)
         pair_ref[:, pl.ds(at + hd, hd)] = val_acc[...].astype(jnp.bfloat16)
 
+    half = blocks // 2
+    quarter = half // 4
+
+    def near_copy(way):
+        return remote(
+            near_out.at[way], near_in.at[way], near_sent.at[way], near_got.at[way], partner
+        )
+
+    def first_copy(way):
+        peer = jnp.where(way == 0, near[0], near[1])
+        return remote(
+            first_out.at[way], first_in.at[way], first_sent.at[way], first_got.at[way], peer
+        )
+
+    def first_part(way):
+        goal = lax.rem(jnp.where(way == 0, spot + chips - 1, spot + 1), chips)
+
+        def product(u, owner):
+            group, split = part(goal, owner)
+            left = tokt[pl.ds(way * half + u * quarter, quarter), split]
+            lanes = pl.ds(pl.multiple_of(group * lane, lane), lane)
+            return jnp.dot(
+                left.reshape(quarter * rows, tok_count), pair_ref[:, lanes],
+                preferred_element_type=jnp.float32,
+            ).reshape(quarter, rows, lane)
+
+        for u in range(4):
+            at = slice(u * quarter, (u + 1) * quarter)
+            near_out[way, at] = product(u, 1 - core).astype(jnp.bfloat16)
+        near_copy(way).start()
+        for u in range(4):
+            at = slice(u * quarter, (u + 1) * quarter)
+            mine = product(u, core)
+            if u == 0:
+                near_copy(way).wait_recv()
+            first_out[way, at] = (mine + near_in[way, at].astype(jnp.float32)).astype(jnp.bfloat16)
+
     tiles = tok_count // tile
-    if groups == chips and heads == hops and subs % tiles == 0:
+    if groups == chips and heads == hops >= 4 and subs % tiles == 0:
         def head_at(k):
             side = jnp.where(lax.rem(k + spot, 2) == 0, 1, -1)
             return lax.rem(spot // 2 + side * ((k + 1) // 2) + 2 * heads, heads)
@@ -289,6 +332,15 @@
             @pl.when(t >= 1)
             def _():
                 finish(head)
+
+            @pl.when((t == hops - 3) | (t == hops - 2))
+            def _():
+                first_part(jnp.where(t == hops - 3, 1 - lax.rem(spot, 2), lax.rem(spot, 2)))
+
+            @pl.when(t == hops - 2)
+            def _():
+                for way in range(2):
+                    first_copy(way).start()
     else:
         @pl.loop(0, hops)
         def _(t):
@@ -309,6 +361,20 @@
 
             finish(head)
 
+        @pl.loop(0, 2)
+        def _(way):
+            first_part(way)
+            first_copy(way).start()
+
+    for way in range(2):
+        first_copy(way).wait_recv()
+    save_first = pltpu.make_async_copy(first_in, first_hbm, save_sem.at[groups + 1])
+    save_first.start()
+
+    for way in range(2):
+        near_copy(way).wait_send()
+        first_copy(way).wait_send()
+
     @pl.loop(1, dp_count)
     def _(k):
         swap_copy(k).wait_send()
@@ -331,10 +397,12 @@
         save_copy(group).wait()
 
     save_tok.wait()
+    save_first.wait()
 
 
 def gather_attend(place, slots, tokens, queries, out_grad, seg_row, head_count, dp_count):
-    slot_count, _, width = slots.shape
+    slot_count = slots.shape[0]
+    width = slots.shape[2] * slots.shape[3]
     tok_count = queries.shape[0]
     q_width = queries.shape[1] * queries.shape[2]
     chips = dp_count // 2
@@ -348,6 +416,7 @@
     tile = 128
     powers = np.power(500000.0, -2.0 * np.arange(lane // 2) / lane)
     frequency = np.concatenate([powers, powers]).astype(np.float32)[None, :]
+    early = (2, blocks // 2, rows, lane)
     turned = (queries.shape[1], tok_count, lane)
     bf = jnp.bfloat16
     f32 = jnp.float32
@@ -361,14 +430,15 @@
             jax.ShapeDtypeStruct((tok_count, width), bf),
             jax.ShapeDtypeStruct((groups, blocks, splits, rows, lane), bf),
             jax.ShapeDtypeStruct((blocks, splits, rows, tok_count), bf),
+            jax.ShapeDtypeStruct(early, bf),
         ),
         in_specs=[pl.BlockSpec(memory_space=pltpu.SMEM), whole, far, far, far, whole, whole],
-        out_specs=(whole, whole, far, far),
+        out_specs=(whole, whole, far, far, far),
         scratch_shapes=[
             pltpu.VMEM(tokens.shape, bf),
             pltpu.VMEM(turned, bf),
             pltpu.VMEM(turned, bf),
-            pltpu.VMEM((2, tile) + queries.shape[1:], bf),
+            pltpu.VMEM((2, tile // 2) + queries.shape[1:], bf),
             pltpu.VMEM((blocks, splits, rows, tok_count), bf),
             pltpu.VMEM((groups, blocks, splits, rows, lane), bf),
             pltpu.VMEM((dp_count, slot_count, rows, lane), bf),
@@ -382,13 +452,22 @@
             pltpu.VMEM((tok_count, lane), f32),
             dma,
             dma((2,)),
-            dma((groups + 1,)),
+            dma((groups + 2,)),
             dma((dp_count,)),
             dma((dp_count,)),
             dma((2, hops, subs)),
             dma((2, hops, subs)),
             dma((chips, subs)),
             dma((chips, subs)),
+            pltpu.VMEM(early, bf),
+            pltpu.VMEM(early, bf),
+            pltpu.VMEM(early, bf),
+            pltpu.VMEM(early, bf),
+            dma((2,)),
+            dma((2,)),
+            dma((2,)),
+            dma((2,)),
+            pltpu.VMEM((slot_count, BR, width), bf),
         ],
         compiler_params=pltpu.CompilerParams(
             collective_id=1, has_side_effects=True, vmem_limit_bytes=VMEM_LIMIT
@@ -402,7 +481,7 @@
 
 
 def scatter_kernel(
-    chips, mp_count, subs, block_of, used, tok_hbm, pair_ref, w_hbm, out_ref, in_ref, tok_ref,
+    chips, mp_count, subs, block_of, used, tok_hbm, pair_ref, first_ref, w_hbm, out_ref, in_ref, tok_ref,
     part_out, part_in, ring_out, ring_in, ready, final, swap_out, swap_in, wbuf, side_out, side_in,
     part_sent, part_got, ring_sent, ring_got, swap_sent, swap_got, tok_sem, load_sem, side_sent, side_got,
 ):
@@ -476,7 +555,7 @@
         return slice(u * size, (u + 1) * size)
 
     def part_fill(step, way, u):
-        part_out[way, lax.rem(step, keep), span(u)] = product(way, step, 1 - core, u).astype(
+        part_out[way, step % keep, span(u)] = product(way, step, 1 - core, u).astype(
             jnp.bfloat16
         )
 
@@ -504,7 +583,7 @@
                         jnp.bfloat16
                     )
                 else:
-                    @pl.when(step >= 2)
+                    @pl.when(step >= 3)
                     def _():
                         ring_copy(way, step - 2, u).wait_send()
 
@@ -558,34 +637,36 @@
         load.wait()
     for way in range(2):
         for u in range(subs):
-            part_fill(0, way, u)
-        part_copy(way, 0).start()
+            part_fill(1, way, u)
+        part_copy(way, 1).start()
     for way in range(2):
         for u in range(subs):
-            ready[way, span(u)] = product(way, 0, core, u)
+            ready[way, span(u)] = product(way, 1, core, u) + first_ref[way, span(u)].astype(
+                jnp.float32
+            )
     for way in range(2):
-        part_copy(way, 0).wait_recv()
+        part_copy(way, 1).wait_recv()
     for u in range(subs):
         for way in range(2):
-            total = ready[way, span(u)] + part_in[way, 0, span(u)].astype(jnp.float32)
-            ring_out[way, 0, span(u)] = total.astype(jnp.bfloat16)
-            ring_copy(way, 0, u).start()
-    for step in range(1, early + 1):
+            total = ready[way, span(u)] + part_in[way, 1, span(u)].astype(jnp.float32)
+            ring_out[way, 1, span(u)] = total.astype(jnp.bfloat16)
+            ring_copy(way, 1, u).start()
+    for step in range(2, early + 2):
         for way in range(2):
             for u in range(subs):
                 part_fill(step, way, u)
             part_copy(way, step).start()
     for way in range(2):
-        part_copy(way, 1).wait_recv()
+        part_copy(way, 2).wait_recv()
         for u in range(subs):
-            ready_fill(1, way, u)
+            ready_fill(2, way, u)
     pace = 2
 
-    @pl.loop(1, chips - 1)
+    @pl.loop(2, chips - 1)
     def _(step):
         ring_step(step, False)
 
-        @pl.loop((step - 1) * pace, step * pace)
+        @pl.loop((step - 2) * pace, (step - 1) * pace)
         def _(k):
             @pl.when(k < units)
             def _():
@@ -618,7 +699,7 @@
     fill(me)
     place_in(me, swap_out[me])
 
-    @pl.loop(min((chips - 2) * pace, units), units)
+    @pl.loop(min((chips - 3) * pace, units), units)
     def _(k):
         unit(k)
 
@@ -636,19 +717,19 @@
     def _(k):
         side_copy(k).wait_send()
 
-    @pl.loop(max(chips - keep, 0), chips)
+    @pl.loop(chips - keep, chips)
     def _(step):
         for way in range(2):
             part_copy(way, step).wait_send()
 
-    @pl.loop(max(chips - 3, 0), chips - 1)
+    @pl.loop(chips - 3, chips - 1)
     def _(step):
         for way in range(2):
             for u in range(subs):
                 ring_copy(way, step, u).wait_send()
 
 
-def scatter_sum(tok_pieces, pairs, gathered, block_of, used, dp_count, mp_count):
+def scatter_sum(tok_pieces, pairs, first, gathered, block_of, used, dp_count, mp_count):
     chips = dp_count // 2
     width = pairs.shape[1]
     blocks, splits, rows, tok_count = tok_pieces.shape
@@ -671,7 +752,7 @@
             jax.ShapeDtypeStruct((slots * BR * groups, lane), jnp.float32),
             jax.ShapeDtypeStruct((tok_count, features), bf),
         ),
-        in_specs=[scalars, scalars, far, whole, far],
+        in_specs=[scalars, scalars, far, whole, whole, far],
         out_specs=(whole, whole),
         scratch_shapes=[
             pltpu.VMEM(tok_pieces.shape, bf),
@@ -704,7 +785,7 @@
             flops=16 * tok_pieces.size * width, bytes_accessed=10**8, transcendentals=0
         ),
         name="scatter_sum",
-    )(block_of, used, tok_pieces, pairs, gathered)
+    )(block_of, used, tok_pieces, pairs, first, gathered)
 
 
 def local(tokens, queries, out_grad, segment_ids, weight_slots, old_place, new_place):
@@ -716,8 +797,8 @@
     slot_total = dp_count * (slot_rows // BR)
     block_count = old_place.shape[0]
 
-    query_grad, pair_grad, gathered, tok_pieces = gather_attend(
-        old_place, weight_slots.reshape(slot_rows // BR, BR, width), tokens,
+    query_grad, pair_grad, gathered, tok_pieces, first = gather_attend(
+        old_place, weight_slots.reshape(slot_rows // BR, BR, 2 * head_count, head_size), tokens,
         queries, out_grad, segment_ids, head_count, dp_count,
     )
     gathered = gathered.reshape(2 * head_count, block_count * BR, head_size)
@@ -727,7 +808,7 @@
     block_of = jnp.sum(matched * jnp.arange(block_count, dtype=jnp.int32)[None, :], axis=1)
     used = jnp.sum(matched, axis=1)
     weight_grad, input_grad = scatter_sum(
-        tok_pieces, pair_grad, gathered, block_of, used, dp_count, mp_count
+        tok_pieces, pair_grad, first, gathered, block_of, used, dp_count, mp_count
     )
     return (
         input_grad,

time: 310 us -> 296 us (0.955)
  Pallas kernels: 292 us -> 283 us
  local copies, waits for them, and re-layouts: 15 us -> 10.6 us
    pallas_call x1, Pallas kernels: 143 us -> 132 us  [scatter_sum(): pl.pallas_call(functools.partial(scatter_kernel, chips, mp_count, subs),...]
    reshape x1 -> x0, local copies, waits for them, and re-layouts: 4.43 us -> none  [local(): weight_slots.reshape(slot_rows // BR, BR, width)]
where the time goes in v4:
time: 296 us; the launch traced here: 295 us
  Pallas kernels  283 us (96%)
  local copies, waits for them, and re-layouts  10.6 us (4%)
    pallas_call x1, Pallas kernels, gather_attend(): pl.pallas_call(functools.partial(gather_kernel, chips, head_count, subs,...  151 us
    pallas_call x1, Pallas kernels, scatter_sum(): pl.pallas_call(functools.partial(scatter_kernel, chips, mp_count, subs),...  132 us
    unnamed x7, local copies, waits for them, and re-layouts  10.6 us

profile of v4, /device:TPU:11, one launch (start us, length us, event | category | flops | bytes accessed | tf_op | source)
XLA Modules:
  0.0 295.4 jit_solution(875362898722885565)
XLA Ops:
  0.6 1.3 convert_reduce_fusion
  1.9 150.7 %gather_attend.1 = (bf16[512,32,128]{2,1,0:T(8,128)(2,1)}, bf16[512,1024]{1,0:T(8,128)(2,1)}, bf16[8,64,2,64,128]{4,3,2,1,0:T(8,128)(2,1)}, bf16[64,2,64,512]{3,2,1,0:T(8,128)(2,1)}, bf16[2,32,64,128]{3,2,1,0:T(8,128)(2,1)}) custom-call(s32[64]{0:T(128)} %place.1, bf16[8,128,8,128]{3,2,1,0:T(8,128)(2,1)} %bitcast.4, bf16[512,8192]{1,0:T(8,128)(2,1)} %tok_hbm.1, ...), custom_call_target="tpu_custom_call" | custom-call | flops 10737418240 | bytes 100000000 | tf_op jit(solution)/shard_map/gather_attend/pallas_call | solution.py:426
  152.6 132.3 %scatter_sum.1 = (f32[8192,128]{1,0:T(8,128)}, bf16[512,4096]{1,0:T(8,128)(2,1)}) custom-call(s32[128]{0:T(128)} %get-tuple-element.18.block_of, s32[128]{0:T(128)} %get-tuple-element.17.used, bf16[64,2,64,512]{3,2,1,0:T(8,128)(2,1)} %get-tuple-element.10.tok_hbm, bf16[512,1024]{1,0:T(8,128)(2,1)} %get-tuple-element.11.pair_ref, ...), custom_call_target="tpu_custom_call" | custom-call | flops 68719476736 | bytes 100000000 | tf_op jit(solution)/shard_map/scatter_sum/pallas_call | solution.py:749
  284.9 0.0 copy-start
  284.9 4.8 %copy.14 = bf16[512,4096]{1,0:T(8,128)(2,1)} copy(bf16[512,4096]{1,0:T(8,128)(2,1)} %get-tuple-element.22) | data formatting | bytes 8388608
  289.7 0.0 copy-done
  289.7 0.0 copy-start.1
  289.7 2.1 copy.15
  291.9 1.6 copy-done.1
  293.4 2.0 copy.16
Async XLA Ops:
  284.9 4.9 %copy-start = (bf16[512,32,128]{2,1,0:T(8,128)(2,1)S(1)}, bf16[512,32,128]{2,1,0:T(8,128)(2,1)}, u32[]{:S(2)}) copy-start(bf16[512,32,128]{2,1,0:T(8,128)(2,1)} %get-tuple-element.23) | copy-start | bytes 12582916
  289.7 3.7 %copy-start.1 = (f32[8192,128]{1,0:T(8,128)S(1)}, f32[8192,128]{1,0:T(8,128)}, u32[]{:S(2)}) copy-start(f32[8192,128]{1,0:T(8,128)} %get-tuple-element.16) | copy-start | bytes 12582916
